TPU v7x, 8 devices: a whole 2x2x1 slice. The times are simulated.
8 devices in a mesh: dp: 1 (over z), tp: 8 (over y, x, core).
Axes of the slice: x: 2, y: 2, z: 1, core: 2. Of those that a mesh axis runs over, the one named last changes fastest.
Arguments:
- hidden: bfloat16 [256, 4096], P('dp')
- positions: int32 [256], P('dp')
- k_cache: bfloat16 [2, 256, 128, 8, 128], P(None, 'dp', None, 'tp')
- v_cache: bfloat16 [2, 256, 128, 8, 128], P(None, 'dp', None, 'tp')
- attn_norm: bfloat16 [2, 4096], replicated
- w_query: bfloat16 [2, 4096, 4096], P(None, None, 'tp')
- w_key: bfloat16 [2, 4096, 1024], P(None, None, 'tp')
- w_value: bfloat16 [2, 4096, 1024], P(None, None, 'tp')
- w_out: bfloat16 [2, 4096, 4096], P(None, 'tp')
- mlp_norm: bfloat16 [2, 4096], replicated
- w_gate: bfloat16 [2, 4096, 14336], P(None, None, 'tp')
- w_up: bfloat16 [2, 4096, 14336], P(None, None, 'tp')
- w_down: bfloat16 [2, 14336, 4096], P(None, 'tp')
Outputs:
- output 1: bfloat16 [256, 4096], P('dp')
- output 2: bfloat16 [2, 256, 128, 8, 128], P(None, 'dp', None, 'tp')
- output 3: bfloat16 [2, 256, 128, 8, 128], P(None, 'dp', None, 'tp')
All inputs are finite; a program needn't handle non-finite values.
Results may differ from a plain program's by a relative error of at most 0.02.
Values are sent between devices in bfloat16 or wider.
A program may use at most 1 GiB of HBM per device.

v0:
```python
import functools
import math
import jax
import jax.numpy as jnp
from jax import lax
from jax.experimental import pallas as pl
from jax.experimental.pallas import tpu as pltpu
from jax.sharding import PartitionSpec as P

MESH = pl.DeviceIdType.MESH
F32 = jnp.float32
BF16 = jnp.bfloat16
ANY = pl.BlockSpec(memory_space=pl.ANY)
VMEM = pl.BlockSpec(memory_space=pltpu.VMEM)
SMEM = pl.BlockSpec(memory_space=pltpu.SMEM)

B = 256
D = 4096
S = 128
HD = 128
G = 4
QW = G * HD
NP = 8
PW = D // NP
FW = 1792
HB = B // 2

CB = 16
NCH = B // CB
NS = 6


def rope_tables(positions):
    half = HD // 2
    inv_freq = jnp.power(500000.0, -jnp.arange(half, dtype=F32) * (2.0 / HD))
    wavelen = (2.0 * math.pi) / inv_freq
    smooth = (8192.0 / wavelen - 1.0) / 3.0
    blended = (1.0 - smooth) * inv_freq / 8.0 + smooth * inv_freq
    scaled = jnp.where(wavelen < 2048.0, inv_freq, jnp.where(wavelen > 8192.0, inv_freq / 8.0, blended))
    angles = positions.astype(F32)[:, None] * scaled[None, :]
    c, s = jnp.cos(angles), jnp.sin(angles)
    return jnp.concatenate([c, c], axis=1), jnp.concatenate([-s, s], axis=1)


def norm_rows(x_ref, h_ref, w_ref, rows=32):
    def step(i, carry):
        sl = pl.ds(pl.multiple_of(i * rows, rows), rows)
        acc = jnp.zeros((rows, 128), F32)
        for c in range(D // 128):
            t = x_ref[sl, c * 128:(c + 1) * 128].astype(F32)
            acc = acc + t * t
        r = lax.rsqrt(jnp.sum(acc, axis=1, keepdims=True) * (1.0 / D) + 1e-5)
        for c in range(D // 512):
            cs = slice(c * 512, (c + 1) * 512)
            h_ref[sl, cs] = (x_ref[sl, cs].astype(F32) * r * w_ref[:, cs].astype(F32)).astype(BF16)
        return carry
    lax.fori_loop(0, B // rows, step, 0, unroll=2)


def attn_kernel(layer, first, pos_ref, x_hbm, nw_ref, cos_ref, sin_ref, wq_hbm, wk_hbm, wv_hbm, kc_hbm, vc_hbm, *rest):
    if first:
        o_ref, ko_hbm, vo_hbm = rest[:3]
        rest = rest[3:]
    else:
        o_ref, ko_hbm, vo_hbm = rest[2:5]
        rest = rest[5:]
    x_v, h_v, wq_v, wk_v, wv_v, acc, q4, o4, kn, vn, rid, kb, vb, wsem, xsem, ksem, vsem, kosem, vosem = rest

    def kv_in(c, slot):
        rs = pl.ds(c * CB, CB)
        return (pltpu.make_async_copy(kc_hbm.at[layer, rs], kb.at[slot], ksem.at[slot]),
                pltpu.make_async_copy(vc_hbm.at[layer, rs], vb.at[slot], vsem.at[slot]))

    def kv_out(c, slot):
        rs = pl.ds(c * CB, CB)
        return (pltpu.make_async_copy(kb.at[slot], ko_hbm.at[layer, rs], kosem.at[slot]),
                pltpu.make_async_copy(vb.at[slot], vo_hbm.at[layer, rs], vosem.at[slot]))

    xcopy = pltpu.make_async_copy(x_hbm, x_v, xsem)
    xcopy.start()
    KC = D // 4
    wcopies = []
    for c in range(4):
        rs = pl.ds(c * KC, KC)
        cs = [pltpu.make_async_copy(wq_hbm.at[layer, rs], wq_v.at[rs], wsem.at[c, 0]),
              pltpu.make_async_copy(wk_hbm.at[layer, rs], wk_v.at[rs], wsem.at[c, 1]),
              pltpu.make_async_copy(wv_hbm.at[layer, rs], wv_v.at[rs], wsem.at[c, 2])]
        for t in cs:
            t.start()
        wcopies.append(cs)
    for c in range(NS - 2):
        for t in kv_in(c, c):
            t.start()

    rid[...] = lax.broadcasted_iota(jnp.int32, (S, HD), 0).astype(F32).astype(BF16)
    xcopy.wait()
    norm_rows(x_v, h_v, nw_ref)
    for c in range(4):
        for t in wcopies[c]:
            t.wait()
        rs = slice(c * KC, (c + 1) * KC)
        w = jnp.concatenate([wq_v[rs, :], wk_v[rs, :], wv_v[rs, :]], axis=1)
        r = jnp.dot(h_v[:, rs], w, preferred_element_type=F32)
        if c == 0:
            acc[...] = r
        else:
            acc[...] += r

    cos = cos_ref[...]
    sin = sin_ref[...]

    def rope(t):
        t = t.astype(BF16).astype(F32)
        return (t * cos + pltpu.roll(t, HD // 2, 1) * sin).astype(BF16).astype(F32)

    for hd in range(G):
        q4[pl.ds(hd, B, stride=G), :] = rope(acc[:, hd * HD:(hd + 1) * HD])
    kn[...] = rope(acc[:, QW:QW + HD])
    vn[...] = acc[:, QW + HD:QW + 2 * HD].astype(BF16).astype(F32)

    scale = HD ** -0.5
    row = lax.broadcasted_iota(jnp.int32, (4 * G, HD), 0) // G
    lane = lax.broadcasted_iota(jnp.int32, (4 * G, HD), 1)
    even = (row % 2) == 0
    low = row < 2

    def chunk(c, carry):
        slot = c % NS
        for t in kv_in(c, slot):
            t.wait()
        rowid = rid[...]
        for g in range(CB // 4):
            b0 = c * CB + 4 * g
            ks, vs = [], []
            posr = jnp.zeros((4 * G, HD), jnp.int32)
            for i in range(4):
                p = pos_ref[b0 + i]
                posr = jnp.where(row == i, p, posr)
                hit = rowid == jnp.full((S, HD), p.astype(F32), F32).astype(BF16)
                kr = jnp.broadcast_to(kn[pl.ds(b0 + i, 1), :], (S, HD)).astype(BF16)
                vr = jnp.broadcast_to(vn[pl.ds(b0 + i, 1), :], (S, HD)).astype(BF16)
                k = jnp.where(hit, kr, kb[slot, 4 * g + i])
                v = jnp.where(hit, vr, vb[slot, 4 * g + i])
                kb[slot, 4 * g + i] = k
                vb[slot, 4 * g + i] = v
                ks.append(k)
                vs.append(v)
            q = q4[pl.ds(pl.multiple_of(b0 * G, 4 * G), 4 * G), :]
            lhs = jnp.concatenate([jnp.where(even, q, 0.0), jnp.where(even, 0.0, q)], axis=1).astype(BF16)
            kt = jnp.concatenate([jnp.concatenate(ks[:2], axis=1), jnp.concatenate(ks[2:], axis=1)], axis=0)
            s2 = lax.dot_general(lhs, kt, (((1,), (1,)), ((), ())), preferred_element_type=F32)
            s = jnp.where(low, s2[:, :S], s2[:, S:]) * scale
            s = jnp.where(lane <= posr, s, -jnp.inf)
            m = jnp.max(s, axis=1, keepdims=True)
            e = jnp.exp(s - m)
            p = e / jnp.sum(e, axis=1, keepdims=True)
            lhs = jnp.concatenate([jnp.where(low, p, 0.0), jnp.where(low, 0.0, p)], axis=1).astype(BF16)
            vt = jnp.concatenate([jnp.concatenate(vs[:2], axis=1), jnp.concatenate(vs[2:], axis=1)], axis=0)
            o2 = jnp.dot(lhs, vt, preferred_element_type=F32)
            o4[pl.ds(pl.multiple_of(b0 * G, 4 * G), 4 * G), :] = jnp.where(even, o2[:, :HD], o2[:, HD:])
        for t in kv_out(c, slot):
            t.start()
        nxt = c + NS - 2
        ns = nxt % NS

        @pl.when(nxt < NCH)
        def _():
            @pl.when(nxt >= NS)
            def _():
                for t in kv_out(nxt - NS, ns):
                    t.wait()
            for t in kv_in(nxt, ns):
                t.start()
        return carry

    lax.fori_loop(0, NCH, chunk, 0)
    for hd in range(G):
        o_ref[:, hd * HD:(hd + 1) * HD] = o4[pl.ds(hd, B, stride=G), :].astype(BF16)
    for c in range(NCH - NS, NCH):
        for t in kv_out(c, c % NS):
            t.wait()


def attn_call(layer, pos, x, nw, cos, sin, wq, wk, wv, kc, vc, prev):
    first = prev is None
    cache = jax.ShapeDtypeStruct(kc.shape, BF16)
    ins = [pos, x, nw, cos, sin, wq, wk, wv, kc, vc]
    specs = [SMEM, ANY, VMEM, VMEM, VMEM] + [ANY] * 5
    alias = {}
    if not first:
        alias = {len(ins): 1, len(ins) + 1: 2}
        ins += list(prev)
        specs += [ANY, ANY]
    return pl.pallas_call(
        functools.partial(attn_kernel, layer, first),
        name=f"attn{layer}",
        out_shape=(jax.ShapeDtypeStruct((B, QW), BF16), cache, cache),
        in_specs=specs,
        out_specs=(VMEM, ANY, ANY),
        scratch_shapes=[
            pltpu.VMEM((B, D), BF16),
            pltpu.VMEM((B, D), BF16),
            pltpu.VMEM((D, QW), BF16),
            pltpu.VMEM((D, HD), BF16),
            pltpu.VMEM((D, HD), BF16),
            pltpu.VMEM((B, QW + 2 * HD), F32),
            pltpu.VMEM((B * G, HD), F32),
            pltpu.VMEM((B * G, HD), F32),
            pltpu.VMEM((B, HD), F32),
            pltpu.VMEM((B, HD), F32),
            pltpu.VMEM((S, HD), BF16),
            pltpu.VMEM((NS, CB, S, HD), BF16),
            pltpu.VMEM((NS, CB, S, HD), BF16),
            pltpu.SemaphoreType.DMA((4, 3)),
            pltpu.SemaphoreType.DMA,
            pltpu.SemaphoreType.DMA((NS,)),
            pltpu.SemaphoreType.DMA((NS,)),
            pltpu.SemaphoreType.DMA((NS,)),
            pltpu.SemaphoreType.DMA((NS,)),
        ],
        input_output_aliases=alias,
        compiler_params=pltpu.CompilerParams(vmem_limit_bytes=60 * 2 ** 20),
    )(*ins)


def mlp_kernel(layer, o_ref, x_hbm, nw_ref, wo_hbm, wg_hbm, wu_hbm, wd_hbm, xo_hbm,
               wo_v, wg_v, wu_v, wd_v, part, xg, h_v, a_v, xown, d2d, r1, r2, wsem, xsem, ssem, rsem):
    me = lax.axis_index("tp")
    k = me % 2
    cx = (me // 2) % 2
    cy = me // 4
    pt = me + 1 - 2 * k
    xn = me + 2 - 4 * cx
    yn = me + 4 - 8 * cy
    dg = xn + 4 - 8 * cy

    def other(p):
        return p + 1 - 2 * k

    def pcols(p):
        return pl.ds(pl.multiple_of(p * PW, PW), PW)

    top = pl.ds(0, HB)
    bot = pl.ds(HB, HB)

    barrier = pltpu.get_barrier_semaphore()
    for d in (pt, xn, yn):
        pl.semaphore_signal(barrier, inc=1, device_id={"tp": d}, device_id_type=MESH)

    xc = pltpu.make_async_copy(x_hbm.at[:, pcols(me)], xown, xsem)
    xc.start()
    wcs = [pltpu.make_async_copy(wo_hbm.at[layer], wo_v, wsem.at[0])]
    NG = 4
    for i in range(NG):
        rs = pl.ds(i * (D // NG), D // NG)
        wcs.append(pltpu.make_async_copy(wg_hbm.at[layer, rs], wg_v.at[rs], wsem.at[1 + 2 * i]))
        wcs.append(pltpu.make_async_copy(wu_hbm.at[layer, rs], wu_v.at[rs], wsem.at[2 + 2 * i]))
    ND = 4
    for i in range(ND):
        rs = pl.ds(i * (FW // ND), FW // ND)
        wcs.append(pltpu.make_async_copy(wd_hbm.at[layer, rs], wd_v.at[rs], wsem.at[1 + 2 * NG + i]))
    for t in wcs:
        t.start()
    pl.semaphore_wait(barrier, 3)

    def send(src, dst, i, dev):
        c = pltpu.make_async_remote_copy(src_ref=src, dst_ref=dst, send_sem=ssem.at[i], recv_sem=rsem.at[i],
                                         device_id={"tp": dev}, device_id_type=MESH)
        c.start()
        return c

    def all_reduce(piece):
        order = (dg, xn, yn, me)
        dcs = []
        for t, p in enumerate(order):
            q = other(p)
            piece(q)
            dcs.append(send(part.at[q], d2d.at[t], t, pt))
            piece(p)

        def pair(t):
            dcs[t].wait_recv()
            p = order[t]
            part[p] = (part[p].astype(F32) + d2d[t].astype(F32)).astype(BF16)

        pair(0)
        sa0 = send(part.at[dg, top], r1.at[0], 4, xn)
        sb0 = send(part.at[dg, bot], r1.at[2], 5, yn)
        pair(1)
        sa1 = send(part.at[xn, top], r1.at[1], 6, xn)
        pair(2)
        sb1 = send(part.at[yn, bot], r1.at[3], 7, yn)
        sa0.wait_recv()
        part[yn, top] = (part[yn, top].astype(F32) + r1[0].astype(F32)).astype(BF16)
        sa2 = send(part.at[yn, top], r2.at[0], 8, yn)
        sb0.wait_recv()
        part[xn, bot] = (part[xn, bot].astype(F32) + r1[2].astype(F32)).astype(BF16)
        sb2 = send(part.at[xn, bot], r2.at[1], 9, xn)
        pair(3)
        sa1.wait_recv()
        sb1.wait_recv()
        sa2.wait_recv()
        tot = part[me, top].astype(F32) + r1[1].astype(F32) + r2[0].astype(F32)
        new = (xown[top].astype(F32) + tot.astype(BF16).astype(F32)).astype(BF16)
        xown[top] = new
        xg[me, top] = new
        ga0 = send(xg.at[me, top], xg.at[me, top], 10, yn)
        ga1 = send(xg.at[me, top], xg.at[me, top], 11, xn)
        sb2.wait_recv()
        tot = part[me, bot].astype(F32) + r1[3].astype(F32) + r2[1].astype(F32)
        new = (xown[bot].astype(F32) + tot.astype(BF16).astype(F32)).astype(BF16)
        xown[bot] = new
        xg[me, bot] = new
        gb0 = send(xg.at[me, bot], xg.at[me, bot], 12, xn)
        gb1 = send(xg.at[me, bot], xg.at[me, bot], 13, yn)
        gp = [send(xg.at[me], xg.at[me], 14, pt)]
        ga0.wait_recv()
        ga2 = send(xg.at[yn, top], xg.at[yn, top], 15, xn)
        gp.append(send(xg.at[yn, top], xg.at[yn, top], 16, pt))
        gb0.wait_recv()
        gb2 = send(xg.at[xn, bot], xg.at[xn, bot], 17, yn)
        gp.append(send(xg.at[xn, bot], xg.at[xn, bot], 18, pt))
        ga1.wait_recv()
        gp.append(send(xg.at[xn, top], xg.at[xn, top], 19, pt))
        gb1.wait_recv()
        gp.append(send(xg.at[yn, bot], xg.at[yn, bot], 20, pt))
        ga2.wait_recv()
        gp.append(send(xg.at[dg, top], xg.at[dg, top], 21, pt))
        gb2.wait_recv()
        gp.append(send(xg.at[dg, bot], xg.at[dg, bot], 22, pt))
        for c in gp:
            c.wait_recv()
        for c in dcs + [sa0, sb0, sa1, sb1, sa2, sb2, ga0, ga1, gb0, gb1, ga2, gb2] + gp:
            c.wait_send()

    wcs[0].wait()

    def out_piece(p):
        part[p] = jnp.dot(o_ref[...], wo_v[:, pcols(p)], preferred_element_type=F32).astype(BF16)

    xc.wait()
    all_reduce(out_piece)

    rows = 32

    def norm_step(i, carry):
        sl = pl.ds(pl.multiple_of(i * rows, rows), rows)
        acc = jnp.zeros((rows, 128), F32)
        for p in range(NP):
            for c in range(PW // 128):
                t = xg[p, sl, c * 128:(c + 1) * 128].astype(F32)
                acc = acc + t * t
        r = lax.rsqrt(jnp.sum(acc, axis=1, keepdims=True) * (1.0 / D) + 1e-5)
        for p in range(NP):
            cs = slice(p * PW, (p + 1) * PW)
            h_v[sl, cs] = (xg[p, sl].astype(F32) * r * nw_ref[:, cs].astype(F32)).astype(BF16)
        return carry

    lax.fori_loop(0, B // rows, norm_step, 0, unroll=2)

    for t in wcs[1:1 + 2 * NG]:
        t.wait()

    TN = 256

    def gate_up(j, carry):
        cs = pl.ds(pl.multiple_of(j * TN, TN), TN)
        w = jnp.concatenate([wg_v[:, cs], wu_v[:, cs]], axis=1)
        gu = jnp.dot(h_v[...], w, preferred_element_type=F32)
        gt = gu[:, :TN].astype(BF16).astype(F32)
        up = gu[:, TN:].astype(BF16).astype(F32)
        a_v[:, cs] = (gt * (1.0 / (1.0 + jnp.exp(-gt))) * up).astype(BF16)
        return carry

    lax.fori_loop(0, FW // TN, gate_up, 0)

    for t in wcs[1 + 2 * NG:]:
        t.wait()

    def down_piece(p):
        part[p] = jnp.dot(a_v[...], wd_v[:, pcols(p)], preferred_element_type=F32).astype(BF16)

    all_reduce(down_piece)

    ocs = [pltpu.make_async_copy(xg.at[p], xo_hbm.at[:, pl.ds(p * PW, PW)], ssem.at[p]) for p in range(NP)]
    for t in ocs:
        t.start()
    for t in ocs:
        t.wait()


def mlp_call(layer, o, x, nw, wo, wg, wu, wd):
    return pl.pallas_call(
        functools.partial(mlp_kernel, layer),
        name=f"mlp{layer}",
        out_shape=jax.ShapeDtypeStruct((B, D), BF16),
        in_specs=[VMEM, ANY, VMEM, ANY, ANY, ANY, ANY],
        out_specs=ANY,
        scratch_shapes=[
            pltpu.VMEM((QW, D), BF16),
            pltpu.VMEM((D, FW), BF16),
            pltpu.VMEM((D, FW), BF16),
            pltpu.VMEM((FW, D), BF16),
            pltpu.VMEM((NP, B, PW), BF16),
            pltpu.VMEM((NP, B, PW), BF16),
            pltpu.VMEM((B, D), BF16),
            pltpu.VMEM((B, FW), BF16),
            pltpu.VMEM((B, PW), BF16),
            pltpu.VMEM((4, B, PW), BF16),
            pltpu.VMEM((4, HB, PW), BF16),
            pltpu.VMEM((2, HB, PW), BF16),
            pltpu.SemaphoreType.DMA((13,)),
            pltpu.SemaphoreType.DMA,
            pltpu.SemaphoreType.DMA((23,)),
            pltpu.SemaphoreType.DMA((23,)),
        ],
        compiler_params=pltpu.CompilerParams(collective_id=layer, has_side_effects=True, vmem_limit_bytes=67043328),
    )(o, x, nw, wo, wg, wu, wd)


def solution(mesh):
    row_spec = P('dp', None)
    pos_spec = P('dp')
    cache_spec = P(None, 'dp', None, 'tp', None)
    norm_spec = P(None, None)
    col_spec = P(None, None, 'tp')
    split_rows = P(None, 'tp', None)

    def local_step(hidden, positions, k_cache, v_cache, attn_norm, w_query, w_key, w_value, w_out, mlp_norm, w_gate, w_up, w_down):
        cos, sin = rope_tables(positions)
        kc = k_cache.reshape(2, B, S, HD)
        vc = v_cache.reshape(2, B, S, HD)
        x = hidden
        prev = None
        for layer in range(2):
            o, ko, vo = attn_call(layer, positions, x, attn_norm[layer][None, :], cos, sin, w_query, w_key, w_value, kc, vc, prev)
            prev = (ko, vo)
            x = mlp_call(layer, o, x, mlp_norm[layer][None, :], w_out, w_gate, w_up, w_down)
        return x, prev[0].reshape(k_cache.shape), prev[1].reshape(v_cache.shape)

    return jax.shard_map(local_step, mesh=mesh, in_specs=(row_spec, pos_spec, cache_spec, cache_spec, norm_spec, col_spec, col_spec, col_spec, split_rows, norm_spec, col_spec, col_spec, split_rows), out_specs=(row_spec, cache_spec, cache_spec), check_vma=False)
```

profile of v0, /device:TPU:1, one launch (start us, length us, event | category | flops | bytes accessed | tf_op | source)
XLA Modules:
  0.0 242.5 jit_solution(5396912036919291314)
XLA Ops:
  0.7 0.7 convert_element_type.3
  1.3 1.4 fusion.2
  2.8 1.4 fusion.1
  4.2 0.5 fusion
  4.7 0.8 pad_maximum_fusion
  5.6 35.7 %attn0.1 = (bf16[256,512]{1,0:T(8,128)(2,1)}, bf16[2,256,128,128]{3,2,1,0:T(8,128)(2,1)}, bf16[2,256,128,128]{3,2,1,0:T(8,128)(2,1)}) custom-call(s32[256]{0:T(256)} %pos_ref.3, bf16[256,4096]{1,0:T(8,128)(2,1)} %x_hbm.3, bf16[1,4096]{1,0:T(2,128)(2,1)} %get-tuple-element.21.nw_ref, f32[256,128]{1,0:T(8,128)} %get-tuple-element.25.cos_ref, ...), custom_call_target="tpu_custom_call" | custom-call | tf_op jit(solution)/shard_map/attn0/pallas_call | solution.py:194
  41.3 81.5 %mlp0.1.x_hbm = bf16[256,4096]{1,0:T(8,128)(2,1)} custom-call(bf16[256,512]{1,0:T(8,128)(2,1)} %get-tuple-element.9.o_ref, bf16[256,4096]{1,0:T(8,128)(2,1)} %x_hbm.3, bf16[1,4096]{1,0:T(2,128)(2,1)} %get-tuple-element.19.nw_ref, bf16[2,512,4096]{2,1,0:T(8,128)(2,1)} %wo_hbm.3, bf16[2,4096,1792]{2,1,0:T(8,128)(2,1)} %wg_hbm.3, ...), custom_call_target="tpu_custom_call" | custom-call | tf_op jit(solution)/shard_map/mlp0/pallas_call | solution.py:393
  122.8 35.7 %attn1.1 = (bf16[256,512]{1,0:T(8,128)(2,1)}, bf16[2,256,128,128]{3,2,1,0:T(8,128)(2,1)}, bf16[2,256,128,128]{3,2,1,0:T(8,128)(2,1)}) custom-call(s32[256]{0:T(256)} %pos_ref.3, bf16[256,4096]{1,0:T(8,128)(2,1)} %mlp0.1.x_hbm, bf16[1,4096]{1,0:T(2,128)(2,1)} %get-tuple-element.20.nw_ref, ...), custom_call_target="tpu_custom_call", output_to_operand_aliasing={{1}: (10, {}), {2}: (11, {})} | custom-call | tf_op jit(solution)/shard_map/attn1/pallas_call | solution.py:194
  158.5 80.8 %mlp1.1 = bf16[256,4096]{1,0:T(8,128)(2,1)} custom-call(bf16[256,512]{1,0:T(8,128)(2,1)} %get-tuple-element.12.o_ref, bf16[256,4096]{1,0:T(8,128)(2,1)} %mlp0.1.x_hbm, bf16[1,4096]{1,0:T(2,128)(2,1)} %get-tuple-element.18.nw_ref, bf16[2,512,4096]{2,1,0:T(8,128)(2,1)} %wo_hbm.3, bf16[2,4096,1792]{2,1,0:T(8,128)(2,1)} %wg_hbm.3, ...), custom_call_target="tpu_custom_call" | custom-call | tf_op jit(solution)/shard_map/mlp1/pallas_call | solution.py:393
  239.3 3.1 %copy.23 = bf16[256,4096]{1,0:T(8,128)(2,1)} copy(bf16[256,4096]{1,0:T(8,128)(2,1)} %mlp1.1) | data formatting | bytes 4194304
  (1 shorter events, 0.0 us)
where the time goes:
time: 244 us; the launch traced here: 242 us
  Pallas kernels  234 us (96%)
  local copies, waits for them, and re-layouts  5.99 us (2%)
    pallas_call x2, Pallas kernels, mlp_call(): pl.pallas_call(functools.partial(mlp_kernel, layer), name=f'mlp{layer}',...  162 us
    pallas_call x2, Pallas kernels, attn_call(): pl.pallas_call(functools.partial(attn_kernel, layer, first), name=f'attn{...  71.3 us

commit v1 on v0

--- a/solution.py
+++ b/solution.py
@@ -25,9 +25,10 @@
 FW = 1792
 HB = B // 2
 
-CB = 16
+CB = 32
 NCH = B // CB
-NS = 6
+NS = 5
+PF = 3
 
 
 def rope_tables(positions):
@@ -88,7 +89,7 @@
         for t in cs:
             t.start()
         wcopies.append(cs)
-    for c in range(NS - 2):
+    for c in range(PF):
         for t in kv_in(c, c):
             t.start()
 
@@ -120,60 +121,79 @@
 
     scale = HD ** -0.5
     row = lax.broadcasted_iota(jnp.int32, (4 * G, HD), 0) // G
-    lane = lax.broadcasted_iota(jnp.int32, (4 * G, HD), 1)
+    lane = lax.broadcasted_iota(jnp.int32, (CB * G, HD), 1)
     even = (row % 2) == 0
     low = row < 2
 
-    def chunk(c, carry):
+    def place(buf, new, slot, b0, i, rowid):
+        hit = rowid == jnp.full((S, HD), pos_ref[b0 + i].astype(F32), F32).astype(BF16)
+        r = jnp.broadcast_to(new[pl.ds(b0 + i, 1), :], (S, HD)).astype(BF16)
+        t = jnp.where(hit, r, buf[slot, i])
+        buf[slot, i] = t
+        return t
+
+    def quad(ts):
+        return jnp.concatenate([jnp.concatenate(ts[:2], axis=1), jnp.concatenate(ts[2:], axis=1)], axis=0)
+
+    def scores(c):
         slot = c % NS
-        for t in kv_in(c, slot):
-            t.wait()
+        b0 = c * CB
+        kv_in(c, slot)[0].wait()
         rowid = rid[...]
+        out = []
         for g in range(CB // 4):
-            b0 = c * CB + 4 * g
-            ks, vs = [], []
-            posr = jnp.zeros((4 * G, HD), jnp.int32)
+            kt = quad([place(kb, kn, slot, b0, 4 * g + i, rowid) for i in range(4)])
+            q = q4[pl.ds(pl.multiple_of(b0 * G + 4 * G * g, 4 * G), 4 * G), :]
+            lhs = jnp.concatenate([jnp.where(even, q, 0.0), jnp.where(even, 0.0, q)], axis=1).astype(BF16)
+            s2 = lax.dot_general(lhs, kt, (((1,), (1,)), ((), ())), preferred_element_type=F32)
+            out.append(jnp.where(low, s2[:, :S], s2[:, S:]))
+        return jnp.concatenate(out, axis=0)
+
+    def values(c, s):
+        slot = c % NS
+        b0 = c * CB
+        kv_in(c, slot)[1].wait()
+        rowid = rid[...]
+        posr = []
+        for g in range(CB // 4):
+            t = jnp.zeros((4 * G, HD), jnp.int32)
             for i in range(4):
-                p = pos_ref[b0 + i]
-                posr = jnp.where(row == i, p, posr)
-                hit = rowid == jnp.full((S, HD), p.astype(F32), F32).astype(BF16)
-                kr = jnp.broadcast_to(kn[pl.ds(b0 + i, 1), :], (S, HD)).astype(BF16)
-                vr = jnp.broadcast_to(vn[pl.ds(b0 + i, 1), :], (S, HD)).astype(BF16)
-                k = jnp.where(hit, kr, kb[slot, 4 * g + i])
-                v = jnp.where(hit, vr, vb[slot, 4 * g + i])
-                kb[slot, 4 * g + i] = k
-                vb[slot, 4 * g + i] = v
-                ks.append(k)
-                vs.append(v)
-            q = q4[pl.ds(pl.multiple_of(b0 * G, 4 * G), 4 * G), :]
-            lhs = jnp.concatenate([jnp.where(even, q, 0.0), jnp.where(even, 0.0, q)], axis=1).astype(BF16)
-            kt = jnp.concatenate([jnp.concatenate(ks[:2], axis=1), jnp.concatenate(ks[2:], axis=1)], axis=0)
-            s2 = lax.dot_general(lhs, kt, (((1,), (1,)), ((), ())), preferred_element_type=F32)
-            s = jnp.where(low, s2[:, :S], s2[:, S:]) * scale
-            s = jnp.where(lane <= posr, s, -jnp.inf)
-            m = jnp.max(s, axis=1, keepdims=True)
-            e = jnp.exp(s - m)
-            p = e / jnp.sum(e, axis=1, keepdims=True)
-            lhs = jnp.concatenate([jnp.where(low, p, 0.0), jnp.where(low, 0.0, p)], axis=1).astype(BF16)
-            vt = jnp.concatenate([jnp.concatenate(vs[:2], axis=1), jnp.concatenate(vs[2:], axis=1)], axis=0)
+                t = jnp.where(row == i, pos_ref[b0 + 4 * g + i], t)
+            posr.append(t)
+        s = jnp.where(lane <= jnp.concatenate(posr, axis=0), s * scale, -jnp.inf)
+        e = jnp.exp(s - jnp.max(s, axis=1, keepdims=True))
+        p = e / jnp.sum(e, axis=1, keepdims=True)
+        for g in range(CB // 4):
+            vt = quad([place(vb, vn, slot, b0, 4 * g + i, rowid) for i in range(4)])
+            pg = p[4 * G * g:4 * G * (g + 1)]
+            lhs = jnp.concatenate([jnp.where(low, pg, 0.0), jnp.where(low, 0.0, pg)], axis=1).astype(BF16)
             o2 = jnp.dot(lhs, vt, preferred_element_type=F32)
-            o4[pl.ds(pl.multiple_of(b0 * G, 4 * G), 4 * G), :] = jnp.where(even, o2[:, :HD], o2[:, HD:])
-        for t in kv_out(c, slot):
-            t.start()
-        nxt = c + NS - 2
-        ns = nxt % NS
+            o4[pl.ds(pl.multiple_of(b0 * G + 4 * G * g, 4 * G), 4 * G), :] = jnp.where(even, o2[:, :HD], o2[:, HD:])
+
+    def turn(c, j):
+        kv_out(c, c % NS)[j].start()
+        nxt = c + PF
 
         @pl.when(nxt < NCH)
         def _():
             @pl.when(nxt >= NS)
             def _():
-                for t in kv_out(nxt - NS, ns):
-                    t.wait()
-            for t in kv_in(nxt, ns):
-                t.start()
-        return carry
-
-    lax.fori_loop(0, NCH, chunk, 0)
+                kv_out(nxt - NS, nxt % NS)[j].wait()
+            kv_in(nxt, nxt % NS)[j].start()
+
+    s0 = scores(0)
+    turn(0, 0)
+
+    def chunk(c, s):
+        sn = scores(c + 1)
+        values(c, s)
+        turn(c + 1, 0)
+        turn(c, 1)
+        return sn
+
+    sl = lax.fori_loop(0, NCH - 1, chunk, s0)
+    values(NCH - 1, sl)
+    turn(NCH - 1, 1)
     for hd in range(G):
         o_ref[:, hd * HD:(hd + 1) * HD] = o4[pl.ds(hd, B, stride=G), :].astype(BF16)
     for c in range(NCH - NS, NCH):

time: 244 us -> 215 us (0.88)
  Pallas kernels: 234 us -> 205 us
    pallas_call x2, Pallas kernels: 71.3 us -> 42.6 us  [attn_call(): pl.pallas_call(functools.partial(attn_kernel, layer, first), name=f'attn{...]
where the time goes in v1:
time: 215 us; the launch traced here: 214 us
  Pallas kernels  205 us (95%)
  local copies, waits for them, and re-layouts  5.99 us (3%)
    pallas_call x2, Pallas kernels, mlp_call(): pl.pallas_call(functools.partial(mlp_kernel, layer), name=f'mlp{layer}',...  162 us
    pallas_call x2, Pallas kernels, attn_call(): pl.pallas_call(functools.partial(attn_kernel, layer, first), name=f'attn{...  42.6 us

profile of v1, /device:TPU:1, one launch (start us, length us, event | category | flops | bytes accessed | tf_op | source)
XLA Modules:
  0.0 213.7 jit_solution(1984048409106294811)
XLA Ops:
  0.7 0.7 convert_element_type.3
  1.3 1.4 fusion.2
  2.8 1.4 fusion.1
  4.2 0.5 fusion
  4.7 0.8 pad_maximum_fusion
  5.6 21.2 %attn0.1 = (bf16[256,512]{1,0:T(8,128)(2,1)}, bf16[2,256,128,128]{3,2,1,0:T(8,128)(2,1)}, bf16[2,256,128,128]{3,2,1,0:T(8,128)(2,1)}) custom-call(s32[256]{0:T(256)} %pos_ref.3, bf16[256,4096]{1,0:T(8,128)(2,1)} %x_hbm.3, bf16[1,4096]{1,0:T(2,128)(2,1)} %get-tuple-element.21.nw_ref, f32[256,128]{1,0:T(8,128)} %get-tuple-element.25.cos_ref, ...), custom_call_target="tpu_custom_call" | custom-call | tf_op jit(solution)/shard_map/attn0/pallas_call | solution.py:214
  26.8 81.5 %mlp0.1.x_hbm = bf16[256,4096]{1,0:T(8,128)(2,1)} custom-call(bf16[256,512]{1,0:T(8,128)(2,1)} %get-tuple-element.9.o_ref, bf16[256,4096]{1,0:T(8,128)(2,1)} %x_hbm.3, bf16[1,4096]{1,0:T(2,128)(2,1)} %get-tuple-element.19.nw_ref, bf16[2,512,4096]{2,1,0:T(8,128)(2,1)} %wo_hbm.3, bf16[2,4096,1792]{2,1,0:T(8,128)(2,1)} %wg_hbm.3, ...), custom_call_target="tpu_custom_call" | custom-call | tf_op jit(solution)/shard_map/mlp0/pallas_call | solution.py:413
  108.3 21.4 %attn1.1 = (bf16[256,512]{1,0:T(8,128)(2,1)}, bf16[2,256,128,128]{3,2,1,0:T(8,128)(2,1)}, bf16[2,256,128,128]{3,2,1,0:T(8,128)(2,1)}) custom-call(s32[256]{0:T(256)} %pos_ref.3, bf16[256,4096]{1,0:T(8,128)(2,1)} %mlp0.1.x_hbm, bf16[1,4096]{1,0:T(2,128)(2,1)} %get-tuple-element.20.nw_ref, ...), custom_call_target="tpu_custom_call", output_to_operand_aliasing={{1}: (10, {}), {2}: (11, {})} | custom-call | tf_op jit(solution)/shard_map/attn1/pallas_call | solution.py:214
  129.8 80.8 %mlp1.1 = bf16[256,4096]{1,0:T(8,128)(2,1)} custom-call(bf16[256,512]{1,0:T(8,128)(2,1)} %get-tuple-element.12.o_ref, bf16[256,4096]{1,0:T(8,128)(2,1)} %mlp0.1.x_hbm, bf16[1,4096]{1,0:T(2,128)(2,1)} %get-tuple-element.18.nw_ref, bf16[2,512,4096]{2,1,0:T(8,128)(2,1)} %wo_hbm.3, bf16[2,4096,1792]{2,1,0:T(8,128)(2,1)} %wg_hbm.3, ...), custom_call_target="tpu_custom_call" | custom-call | tf_op jit(solution)/shard_map/mlp1/pallas_call | solution.py:413
  210.6 3.1 %copy.23 = bf16[256,4096]{1,0:T(8,128)(2,1)} copy(bf16[256,4096]{1,0:T(8,128)(2,1)} %mlp1.1) | data formatting | bytes 4194304
  (1 shorter events, 0.0 us)

commit v2 on v1

v2 whole, which is shorter than its diff:
```python
import functools
import math
import jax
import jax.numpy as jnp
from jax import lax
from jax.experimental import pallas as pl
from jax.experimental.pallas import tpu as pltpu
from jax.sharding import PartitionSpec as P

MESH = pl.DeviceIdType.MESH
F32 = jnp.float32
BF16 = jnp.bfloat16
ANY = pl.BlockSpec(memory_space=pl.ANY)
VMEM = pl.BlockSpec(memory_space=pltpu.VMEM)
SMEM = pl.BlockSpec(memory_space=pltpu.SMEM)

B = 256
D = 4096
S = 128
HD = 128
G = 4
QW = G * HD
NP = 8
PW = D // NP
FW = 1792
HB = B // 2
PH = PW // 2
NC = 23

CB = 32
NCH = B // CB
NS = 5
PF = 3


def rope_tables(shape):
    half = HD // 2
    lane = lax.broadcasted_iota(jnp.int32, shape, 1)
    index = jnp.where(lane < half, lane, lane - half).astype(F32)
    inv_freq = jnp.exp(index * (-2.0 / HD * math.log(500000.0)))
    wavelen = (2.0 * math.pi) / inv_freq
    smooth = (8192.0 / wavelen - 1.0) / 3.0
    blended = (1.0 - smooth) * inv_freq / 8.0 + smooth * inv_freq
    scaled = jnp.where(wavelen < 2048.0, inv_freq, jnp.where(wavelen > 8192.0, inv_freq / 8.0, blended))
    angles = lax.broadcasted_iota(jnp.int32, shape, 0).astype(F32) * scaled
    return jnp.cos(angles), jnp.where(lane < half, -1.0, 1.0) * jnp.sin(angles)


def norm_rows(x_ref, h_ref, w_ref, layer, rows=32):
    def step(i, carry):
        sl = pl.ds(pl.multiple_of(i * rows, rows), rows)
        acc = jnp.zeros((rows, 128), F32)
        for c in range(D // 128):
            t = x_ref[sl, c * 128:(c + 1) * 128].astype(F32)
            acc = acc + t * t
        r = lax.rsqrt(jnp.sum(acc, axis=1, keepdims=True) * (1.0 / D) + 1e-5)
        for c in range(D // 512):
            cs = slice(c * 512, (c + 1) * 512)
            h_ref[sl, cs] = (x_ref[sl, cs].astype(F32) * r * w_ref[layer:layer + 1, cs].astype(F32)).astype(BF16)
        return carry
    lax.fori_loop(0, B // rows, step, 0, unroll=2)


def attn_kernel(layer, first, pos_ref, x_hbm, nw_ref, wq_hbm, wk_hbm, wv_hbm, kc_hbm, vc_hbm, *rest):
    if first:
        o_ref, ko_hbm, vo_hbm = rest[:3]
        rest = rest[3:]
    else:
        o_ref, ko_hbm, vo_hbm = rest[2:5]
        rest = rest[5:]
    x_v, h_v, cos_t, sin_t, cos_ref, sin_ref, wq_v, wk_v, wv_v, acc, q4, o4, kn, vn, rid, kb, vb, wsem, xsem, ksem, vsem, kosem, vosem = rest

    def kv_in(c, slot):
        rs = pl.ds(c * CB, CB)
        return (pltpu.make_async_copy(kc_hbm.at[layer, rs], kb.at[slot], ksem.at[slot]),
                pltpu.make_async_copy(vc_hbm.at[layer, rs], vb.at[slot], vsem.at[slot]))

    def kv_out(c, slot):
        rs = pl.ds(c * CB, CB)
        return (pltpu.make_async_copy(kb.at[slot], ko_hbm.at[layer, rs], kosem.at[slot]),
                pltpu.make_async_copy(vb.at[slot], vo_hbm.at[layer, rs], vosem.at[slot]))

    xcopy = pltpu.make_async_copy(x_hbm, x_v, xsem)
    xcopy.start()
    KC = D // 4
    wcopies = []
    for c in range(4):
        rs = pl.ds(c * KC, KC)
        cs = [pltpu.make_async_copy(wq_hbm.at[layer, rs], wq_v.at[rs], wsem.at[c, 0]),
              pltpu.make_async_copy(wk_hbm.at[layer, rs], wk_v.at[rs], wsem.at[c, 1]),
              pltpu.make_async_copy(wv_hbm.at[layer, rs], wv_v.at[rs], wsem.at[c, 2])]
        for t in cs:
            t.start()
        wcopies.append(cs)
    for c in range(PF):
        for t in kv_in(c, c):
            t.start()

    rid[...] = lax.broadcasted_iota(jnp.int32, (S, HD), 0).astype(F32).astype(BF16)
    cos_t[...], sin_t[...] = rope_tables((S, HD))

    def look_up(b, carry):
        p = pos_ref[b]
        cos_ref[pl.ds(b, 1), :] = cos_t[pl.ds(p, 1), :]
        sin_ref[pl.ds(b, 1), :] = sin_t[pl.ds(p, 1), :]
        return carry

    lax.fori_loop(0, B, look_up, 0, unroll=8)
    xcopy.wait()
    norm_rows(x_v, h_v, nw_ref, layer)
    for c in range(4):
        for t in wcopies[c]:
            t.wait()
        rs = slice(c * KC, (c + 1) * KC)
        w = jnp.concatenate([wq_v[rs, :], wk_v[rs, :], wv_v[rs, :]], axis=1)
        r = jnp.dot(h_v[:, rs], w, preferred_element_type=F32)
        if c == 0:
            acc[...] = r
        else:
            acc[...] += r

    cos = cos_ref[...]
    sin = sin_ref[...]

    def rope(t):
        t = t.astype(BF16).astype(F32)
        return (t * cos + pltpu.roll(t, HD // 2, 1) * sin).astype(BF16).astype(F32)

    for hd in range(G):
        q4[pl.ds(hd, B, stride=G), :] = rope(acc[:, hd * HD:(hd + 1) * HD])
    kn[...] = rope(acc[:, QW:QW + HD])
    vn[...] = acc[:, QW + HD:QW + 2 * HD].astype(BF16).astype(F32)

    scale = HD ** -0.5
    row = lax.broadcasted_iota(jnp.int32, (4 * G, HD), 0) // G
    lane = lax.broadcasted_iota(jnp.int32, (CB * G, HD), 1)
    even = (row % 2) == 0
    low = row < 2

    def place(buf, new, slot, b0, i, rowid):
        hit = rowid == jnp.full((S, HD), pos_ref[b0 + i].astype(F32), F32).astype(BF16)
        r = jnp.broadcast_to(new[pl.ds(b0 + i, 1), :], (S, HD)).astype(BF16)
        t = jnp.where(hit, r, buf[slot, i])
        buf[slot, i] = t
        return t

    def quad(ts):
        return jnp.concatenate([jnp.concatenate(ts[:2], axis=1), jnp.concatenate(ts[2:], axis=1)], axis=0)

    def scores(c):
        slot = c % NS
        b0 = c * CB
        kv_in(c, slot)[0].wait()
        rowid = rid[...]
        out = []
        for g in range(CB // 4):
            kt = quad([place(kb, kn, slot, b0, 4 * g + i, rowid) for i in range(4)])
            q = q4[pl.ds(pl.multiple_of(b0 * G + 4 * G * g, 4 * G), 4 * G), :]
            lhs = jnp.concatenate([jnp.where(even, q, 0.0), jnp.where(even, 0.0, q)], axis=1).astype(BF16)
            s2 = lax.dot_general(lhs, kt, (((1,), (1,)), ((), ())), preferred_element_type=F32)
            out.append(jnp.where(low, s2[:, :S], s2[:, S:]))
        return jnp.concatenate(out, axis=0)

    def values(c, s):
        slot = c % NS
        b0 = c * CB
        kv_in(c, slot)[1].wait()
        rowid = rid[...]
        posr = []
        for g in range(CB // 4):
            t = jnp.zeros((4 * G, HD), jnp.int32)
            for i in range(4):
                t = jnp.where(row == i, pos_ref[b0 + 4 * g + i], t)
            posr.append(t)
        s = jnp.where(lane <= jnp.concatenate(posr, axis=0), s * scale, -jnp.inf)
        e = jnp.exp(s - jnp.max(s, axis=1, keepdims=True))
        p = e / jnp.sum(e, axis=1, keepdims=True)
        for g in range(CB // 4):
            vt = quad([place(vb, vn, slot, b0, 4 * g + i, rowid) for i in range(4)])
            pg = p[4 * G * g:4 * G * (g + 1)]
            lhs = jnp.concatenate([jnp.where(low, pg, 0.0), jnp.where(low, 0.0, pg)], axis=1).astype(BF16)
            o2 = jnp.dot(lhs, vt, preferred_element_type=F32)
            o4[pl.ds(pl.multiple_of(b0 * G + 4 * G * g, 4 * G), 4 * G), :] = jnp.where(even, o2[:, :HD], o2[:, HD:])

    def turn(c, j):
        kv_out(c, c % NS)[j].start()
        nxt = c + PF

        @pl.when(nxt < NCH)
        def _():
            @pl.when(nxt >= NS)
            def _():
                kv_out(nxt - NS, nxt % NS)[j].wait()
            kv_in(nxt, nxt % NS)[j].start()

    s0 = scores(0)
    turn(0, 0)

    def chunk(c, s):
        sn = scores(c + 1)
        values(c, s)
        turn(c + 1, 0)
        turn(c, 1)
        return sn

    sl = lax.fori_loop(0, NCH - 1, chunk, s0)
    values(NCH - 1, sl)
    turn(NCH - 1, 1)
    for hd in range(G):
        o_ref[:, hd * HD:(hd + 1) * HD] = o4[pl.ds(hd, B, stride=G), :].astype(BF16)
    for c in range(NCH - NS, NCH):
        for t in kv_out(c, c % NS):
            t.wait()


def attn_call(layer, pos, x, nw, wq, wk, wv, kc, vc, prev):
    first = prev is None
    cache = jax.ShapeDtypeStruct(kc.shape, BF16)
    ins = [pos, x, nw, wq, wk, wv, kc, vc]
    specs = [SMEM, ANY, VMEM] + [ANY] * 5
    alias = {}
    if not first:
        alias = {len(ins): 1, len(ins) + 1: 2}
        ins += list(prev)
        specs += [ANY, ANY]
    return pl.pallas_call(
        functools.partial(attn_kernel, layer, first),
        name=f"attn{layer}",
        out_shape=(jax.ShapeDtypeStruct((B, QW), BF16), cache, cache),
        in_specs=specs,
        out_specs=(VMEM, ANY, ANY),
        scratch_shapes=[
            pltpu.VMEM((B, D), BF16),
            pltpu.VMEM((B, D), BF16),
            pltpu.VMEM((S, HD), F32),
            pltpu.VMEM((S, HD), F32),
            pltpu.VMEM((B, HD), F32),
            pltpu.VMEM((B, HD), F32),
            pltpu.VMEM((D, QW), BF16),
            pltpu.VMEM((D, HD), BF16),
            pltpu.VMEM((D, HD), BF16),
            pltpu.VMEM((B, QW + 2 * HD), F32),
            pltpu.VMEM((B * G, HD), F32),
            pltpu.VMEM((B * G, HD), F32),
            pltpu.VMEM((B, HD), F32),
            pltpu.VMEM((B, HD), F32),
            pltpu.VMEM((S, HD), BF16),
            pltpu.VMEM((NS, CB, S, HD), BF16),
            pltpu.VMEM((NS, CB, S, HD), BF16),
            pltpu.SemaphoreType.DMA((4, 3)),
            pltpu.SemaphoreType.DMA,
            pltpu.SemaphoreType.DMA((NS,)),
            pltpu.SemaphoreType.DMA((NS,)),
            pltpu.SemaphoreType.DMA((NS,)),
            pltpu.SemaphoreType.DMA((NS,)),
        ],
        input_output_aliases=alias,
        compiler_params=pltpu.CompilerParams(vmem_limit_bytes=60 * 2 ** 20),
    )(*ins)


def mlp_kernel(layer, o_ref, x_hbm, nw_ref, wo_hbm, wg_hbm, wu_hbm, wd_hbm, xo_hbm,
               wo_v, wg_v, wu_v, wd_v, part, xg, hc, acc, a_v, xown, d2d, r1, r2, ssb, r_v,
               wsem, osem, xsem, ssem, rsem):
    me = lax.axis_index("tp")
    k = me % 2
    cx = (me // 2) % 2
    cy = me // 4
    pt = me + 1 - 2 * k
    xn = me + 2 - 4 * cx
    yn = me + 4 - 8 * cy
    dg = xn + 4 - 8 * cy

    def other(p):
        return p + 1 - 2 * k

    peers = (pt, xn, yn, dg, other(xn), other(yn), other(dg))
    order = (dg, xn, yn, me)
    top = pl.ds(0, HB)
    bot = pl.ds(HB, HB)

    def cols(p, h):
        return pl.ds(pl.multiple_of(p * PW + h * PH, PH), PH)

    def chip_cols(p):
        return pl.ds(pl.multiple_of((p // 2) * 2 * PW, 2 * PW), 2 * PW)

    barrier = pltpu.get_barrier_semaphore()
    for d in peers:
        pl.semaphore_signal(barrier, inc=1, device_id={"tp": d}, device_id_type=MESH)

    wos = [pltpu.make_async_copy(wo_hbm.at[layer, :, chip_cols(p)], wo_v.at[:, chip_cols(p)], osem.at[i]) for i, p in enumerate(order)]
    xcs = [pltpu.make_async_copy(x_hbm.at[:, cols(me, h)], xown.at[h], xsem.at[h]) for h in range(2)]
    NG = 4
    gus = []
    for i in range(NG):
        rs = pl.ds(i * (D // NG), D // NG)
        gus.append(pltpu.make_async_copy(wg_hbm.at[layer, rs], wg_v.at[rs], wsem.at[2 * i]))
        gus.append(pltpu.make_async_copy(wu_hbm.at[layer, rs], wu_v.at[rs], wsem.at[2 * i + 1]))
    ND = 4
    wds = []
    for i in range(ND):
        rs = pl.ds(i * (FW // ND), FW // ND)
        wds.append(pltpu.make_async_copy(wd_hbm.at[layer, rs], wd_v.at[rs], wsem.at[2 * NG + i]))
    for t in wos + xcs + gus + wds:
        t.start()
    pl.semaphore_wait(barrier, len(peers))

    def send(src, dst, i, dev):
        c = pltpu.make_async_remote_copy(src_ref=src, dst_ref=dst, send_sem=ssem.at[i], recv_sem=rsem.at[i],
                                         device_id={"tp": dev}, device_id_type=MESH)
        c.start()
        return c

    def reduce_scatter(make):
        live = [{}, {}]

        def pair(h, t):
            c = live[h]
            p = order[t]
            c["d%d" % t].wait_recv()
            part[h, p] = (part[h, p].astype(F32) + d2d[h, t].astype(F32)).astype(BF16)
            if t == 0:
                c["a0"] = send(part.at[h, dg, top], r1.at[h, 0], NC * h + 4, xn)
                c["b0"] = send(part.at[h, dg, bot], r1.at[h, 2], NC * h + 5, yn)
            elif t == 1:
                c["a1"] = send(part.at[h, xn, top], r1.at[h, 1], NC * h + 6, xn)
            elif t == 2:
                c["b1"] = send(part.at[h, yn, bot], r1.at[h, 3], NC * h + 7, yn)

        todo = []
        for h in range(2):
            for t, p in enumerate(order):
                q = other(p)
                make(h, t, p, q)
                live[h]["d%d" % t] = send(part.at[h, q], d2d.at[h, t], NC * h + t, pt)
                if todo:
                    pair(*todo.pop(0))
                todo.append((h, t))
        pair(*todo.pop(0))
        for h in range(2):
            c = live[h]
            c["a0"].wait_recv()
            part[h, yn, top] = (part[h, yn, top].astype(F32) + r1[h, 0].astype(F32)).astype(BF16)
            c["a2"] = send(part.at[h, yn, top], r2.at[h, 0], NC * h + 8, yn)
            c["b0"].wait_recv()
            part[h, xn, bot] = (part[h, xn, bot].astype(F32) + r1[h, 2].astype(F32)).astype(BF16)
            c["b2"] = send(part.at[h, xn, bot], r2.at[h, 1], NC * h + 9, xn)
        return live

    def final(h, c):
        for rs, a, b, i, j in ((top, "a1", "a2", 1, 0), (bot, "b1", "b2", 3, 1)):
            c[a].wait_recv()
            c[b].wait_recv()
            tot = part[h, me, rs].astype(F32) + r1[h, i].astype(F32) + r2[h, j].astype(F32)
            new = (xown[h, rs].astype(F32) + tot.astype(BF16).astype(F32)).astype(BF16)
            xown[h, rs] = new
            xg[h, me, rs] = new

    def gather_start(h, c):
        def go(name, p, rs, i, dev):
            c[name] = send(xg.at[h, p, rs], xg.at[h, p, rs], NC * h + i, dev)
        go("ga0", me, top, 10, yn)
        go("gb0", me, bot, 11, xn)
        go("ga1", me, top, 12, xn)
        go("gb1", me, bot, 13, yn)
        c["p0"] = send(xg.at[h, me], xg.at[h, me], NC * h + 14, pt)

    def forward(h, c, got, name, p, rs, i):
        c[got].wait_recv()
        c[name] = send(xg.at[h, p, rs], xg.at[h, p, rs], NC * h + i, pt)

    def relay(h, c):
        forward(h, c, "ga0", "p1", yn, top, 15)
        c["ga2"] = send(xg.at[h, yn, top], xg.at[h, yn, top], NC * h + 16, xn)
        forward(h, c, "gb0", "p2", xn, bot, 17)
        c["gb2"] = send(xg.at[h, xn, bot], xg.at[h, xn, bot], NC * h + 18, yn)

    def near(h, c):
        forward(h, c, "ga1", "p3", xn, top, 19)
        forward(h, c, "gb1", "p4", yn, bot, 20)

    def far(h, c):
        forward(h, c, "ga2", "p5", dg, top, 21)
        forward(h, c, "gb2", "p6", dg, bot, 22)

    def drain(live):
        for c in live:
            for t in c.values():
                t.wait_send()

    def got(live, *names):
        for c in live:
            for n in names:
                c[n].wait_recv()

    def out_half(h, i, p, q):
        if h == 0:
            wos[i].wait()
        w = jnp.concatenate([wo_v[:, cols(p, h)], wo_v[:, cols(q, h)]], axis=1)
        t = jnp.dot(o_ref[...], w, preferred_element_type=F32).astype(BF16)
        part[h, p] = t[:, :PH]
        part[h, q] = t[:, PH:]

    live = reduce_scatter(out_half)
    for t in xcs:
        t.wait()
    final(0, live[0])
    gather_start(0, live[0])
    final(1, live[1])
    sq = jnp.zeros((B, 128), F32)
    for h in range(2):
        for c in range(PH // 128):
            t = xg[h, me, :, c * 128:(c + 1) * 128].astype(F32)
            sq = sq + t * t
    ssb[0] = jnp.broadcast_to(jnp.sum(sq.T, axis=0, keepdims=True), (8, B))
    sss = [send(ssb.at[0], ssb.at[1 + j], 2 * NC + j, d) for j, d in enumerate(peers)]
    gather_start(1, live[1])
    relay(0, live[0])
    for t in sss:
        t.wait_recv()
    tot = ssb[0]
    for j in range(len(peers)):
        tot = tot + ssb[1 + j]
    rr = lax.rsqrt(tot * (1.0 / D) + 1e-5)
    r_v[...] = jnp.broadcast_to(rr[0:1], (128, B)).T
    relay(1, live[1])
    for h in range(2):
        near(h, live[h])
    for t in gus:
        t.wait()

    TN = 256

    def gate_up(p, first, last):
        base = pl.multiple_of((p // 2) * 2 * PW, 2 * PW)

        def norm_step(i, carry):
            sl = pl.ds(pl.multiple_of(i * 64, 64), 64)
            r = r_v[sl, :]
            for c in range(2 * PW // 128):
                cs = slice(c * 128, (c + 1) * 128)
                e, h, o = c // 4, (c // 2) % 2, (c % 2) * 128
                w = nw_ref[layer:layer + 1, pl.ds(pl.multiple_of(base + c * 128, 128), 128)].astype(F32)
                hc[sl, cs] = (xg[h, (p // 2) * 2 + e, sl, o:o + 128].astype(F32) * r * w).astype(BF16)
            return carry

        lax.fori_loop(0, B // 64, norm_step, 0)

        def tile(j, carry):
            cs = pl.ds(pl.multiple_of(j * TN, TN), TN)
            ks = pl.ds(base, 2 * PW)
            w = jnp.concatenate([wg_v[ks, cs], wu_v[ks, cs]], axis=1)
            gu = jnp.dot(hc[...], w, preferred_element_type=F32)
            if not first:
                gu = gu + acc[j]
            if not last:
                acc[j] = gu
            else:
                gt = gu[:, :TN].astype(BF16).astype(F32)
                up = gu[:, TN:].astype(BF16).astype(F32)
                a_v[:, cs] = (gt * (1.0 / (1.0 + jnp.exp(-gt))) * up).astype(BF16)
            return carry

        lax.fori_loop(0, FW // TN, tile, 0)

    got(live, "p0")
    gate_up(me, True, False)
    got(live, "p2", "p3")
    gate_up(xn, False, False)
    for h in range(2):
        far(h, live[h])
    got(live, "p1", "p4")
    gate_up(yn, False, False)
    got(live, "p5", "p6")
    gate_up(dg, False, True)
    drain(live)
    for t in sss:
        t.wait_send()
    for t in wds:
        t.wait()

    def down_half(h, i, p, q):
        w = jnp.concatenate([wd_v[:, cols(p, h)], wd_v[:, cols(q, h)]], axis=1)
        t = jnp.dot(a_v[...], w, preferred_element_type=F32).astype(BF16)
        part[h, p] = t[:, :PH]
        part[h, q] = t[:, PH:]

    live = reduce_scatter(down_half)
    for h in range(2):
        final(h, live[h])
        gather_start(h, live[h])
    for h in range(2):
        relay(h, live[h])
    for h in range(2):
        near(h, live[h])
    outs = []

    def write(p):
        for e in range(2):
            for h in range(2):
                n = (p // 2) * 2 + e
                c = pltpu.make_async_copy(xg.at[h, n], xo_hbm.at[:, cols(n, h)], wsem.at[len(outs)])
                c.start()
                outs.append(c)

    got(live, "p0")
    write(me)
    for h in range(2):
        far(h, live[h])
    got(live, "p2", "p3")
    write(xn)
    got(live, "p1", "p4")
    write(yn)
    got(live, "p5", "p6")
    write(dg)
    drain(live)
    for c in outs:
        c.wait()


def mlp_call(layer, o, x, nw, wo, wg, wu, wd):
    return pl.pallas_call(
        functools.partial(mlp_kernel, layer),
        name=f"mlp{layer}",
        out_shape=jax.ShapeDtypeStruct((B, D), BF16),
        in_specs=[VMEM, ANY, VMEM, ANY, ANY, ANY, ANY],
        out_specs=ANY,
        scratch_shapes=[
            pltpu.VMEM((QW, D), BF16),
            pltpu.VMEM((D, FW), BF16),
            pltpu.VMEM((D, FW), BF16),
            pltpu.VMEM((FW, D), BF16),
            pltpu.VMEM((2, NP, B, PH), BF16),
            pltpu.VMEM((2, NP, B, PH), BF16),
            pltpu.VMEM((B, 2 * PW), BF16),
            pltpu.VMEM((FW // 256, B, 512), F32),
            pltpu.VMEM((B, FW), BF16),
            pltpu.VMEM((2, B, PH), BF16),
            pltpu.VMEM((2, 4, B, PH), BF16),
            pltpu.VMEM((2, 4, HB, PH), BF16),
            pltpu.VMEM((2, 2, HB, PH), BF16),
            pltpu.VMEM((8, 8, B), F32),
            pltpu.VMEM((B, 128), F32),
            pltpu.SemaphoreType.DMA((16,)),
            pltpu.SemaphoreType.DMA((4,)),
            pltpu.SemaphoreType.DMA((2,)),
            pltpu.SemaphoreType.DMA((2 * NC + 7,)),
            pltpu.SemaphoreType.DMA((2 * NC + 7,)),
        ],
        compiler_params=pltpu.CompilerParams(collective_id=layer, has_side_effects=True, vmem_limit_bytes=67043328),
    )(o, x, nw, wo, wg, wu, wd)


def solution(mesh):
    row_spec = P('dp', None)
    pos_spec = P('dp')
    cache_spec = P(None, 'dp', None, 'tp', None)
    norm_spec = P(None, None)
    col_spec = P(None, None, 'tp')
    split_rows = P(None, 'tp', None)

    def local_step(hidden, positions, k_cache, v_cache, attn_norm, w_query, w_key, w_value, w_out, mlp_norm, w_gate, w_up, w_down):
        kc = k_cache.reshape(2, B, S, HD)
        vc = v_cache.reshape(2, B, S, HD)
        x = hidden
        prev = None
        for layer in range(2):
            o, ko, vo = attn_call(layer, positions, x, attn_norm, w_query, w_key, w_value, kc, vc, prev)
            prev = (ko, vo)
            x = mlp_call(layer, o, x, mlp_norm, w_out, w_gate, w_up, w_down)
        return x, prev[0].reshape(k_cache.shape), prev[1].reshape(v_cache.shape)

    return jax.shard_map(local_step, mesh=mesh, in_specs=(row_spec, pos_spec, cache_spec, cache_spec, norm_spec, col_spec, col_spec, col_spec, split_rows, norm_spec, col_spec, col_spec, split_rows), out_specs=(row_spec, cache_spec, cache_spec), check_vma=False)
```

time: 215 us -> 191 us (0.89)
  Pallas kernels: 205 us -> 187 us
  local copies, waits for them, and re-layouts: 5.99 us -> 3.13 us
    pallas_call x2, Pallas kernels: 162 us -> 145 us  [mlp_call(): pl.pallas_call(functools.partial(mlp_kernel, layer), name=f'mlp{layer}',...]
    slice x2 -> x0, local copies, waits for them, and re-layouts: 2.86 us -> none  [the longest x1 1.44 us: local_step(): mlp_norm[layer][None, :]]
where the time goes in v2:
time: 191 us
  Pallas kernels  187 us (98%)
  local copies, waits for them, and re-layouts  3.13 us (2%)
    pallas_call x2, Pallas kernels, mlp_call(): pl.pallas_call(functools.partial(mlp_kernel, layer), name=f'mlp{layer}',...  145 us
    pallas_call x2, Pallas kernels, attn_call(): pl.pallas_call(functools.partial(attn_kernel, layer, first), name=f'attn{...  41.9 us

profile of v2, /device:TPU:1, one launch (start us, length us, event | category | flops | bytes accessed | tf_op | source)
XLA Modules:
  0.0 191.0 jit_solution(9595284359895166486)
XLA Ops:
  0.6 21.0 %attn0.1 = (bf16[256,512]{1,0:T(8,128)(2,1)}, bf16[2,256,128,128]{3,2,1,0:T(8,128)(2,1)}, bf16[2,256,128,128]{3,2,1,0:T(8,128)(2,1)}) custom-call(s32[256]{0:T(256)} %pos_ref.3, bf16[256,4096]{1,0:T(8,128)(2,1)} %x_hbm.3, bf16[2,4096]{1,0:T(2,128)(2,1)} %nw_ref.6, bf16[2,4096,512]{2,1,0:T(8,128)(2,1)} %wq_hbm.3, bf16[2,4096,128]{2,1,0:T(8,128)(2,1)} %wk_hbm.3, ...), custom_call_target="tpu_custom_call" | custom-call | tf_op jit(solution)/shard_map/attn0/pallas_call | solution.py:226
  21.6 73.2 %mlp0.1.x_hbm = bf16[256,4096]{1,0:T(8,128)(2,1)} custom-call(bf16[256,512]{1,0:T(8,128)(2,1)} %get-tuple-element.9.o_ref, bf16[256,4096]{1,0:T(8,128)(2,1)} %x_hbm.3, bf16[2,4096]{1,0:T(2,128)(2,1)} %nw_ref.7, bf16[2,512,4096]{2,1,0:T(8,128)(2,1)} %wo_hbm.3, bf16[2,4096,1792]{2,1,0:T(8,128)(2,1)} %wg_hbm.3, bf16[2,4096,1792]{2,1,0:T(8,128)(2,1)} %wu_hbm.3, ...), custom_call_target="tpu_custom_call" | custom-call | tf_op jit(solution)/shard_map/mlp0/pallas_call | solution.py:523
  94.8 21.0 %attn1.1 = (bf16[256,512]{1,0:T(8,128)(2,1)}, bf16[2,256,128,128]{3,2,1,0:T(8,128)(2,1)}, bf16[2,256,128,128]{3,2,1,0:T(8,128)(2,1)}) custom-call(s32[256]{0:T(256)} %pos_ref.3, bf16[256,4096]{1,0:T(8,128)(2,1)} %mlp0.1.x_hbm, bf16[2,4096]{1,0:T(2,128)(2,1)} %nw_ref.6, bf16[2,4096,512]{2,1,0:T(8,128)(2,1)} %wq_hbm.3, ...), custom_call_target="tpu_custom_call", output_to_operand_aliasing={{1}: (8, {}), {2}: (9, {})} | custom-call | tf_op jit(solution)/shard_map/attn1/pallas_call | solution.py:226
  115.8 72.1 %mlp1.1 = bf16[256,4096]{1,0:T(8,128)(2,1)} custom-call(bf16[256,512]{1,0:T(8,128)(2,1)} %get-tuple-element.12.o_ref, bf16[256,4096]{1,0:T(8,128)(2,1)} %mlp0.1.x_hbm, bf16[2,4096]{1,0:T(2,128)(2,1)} %nw_ref.7, bf16[2,512,4096]{2,1,0:T(8,128)(2,1)} %wo_hbm.3, bf16[2,4096,1792]{2,1,0:T(8,128)(2,1)} %wg_hbm.3, bf16[2,4096,1792]{2,1,0:T(8,128)(2,1)} %wu_hbm.3, ...), custom_call_target="tpu_custom_call" | custom-call | tf_op jit(solution)/shard_map/mlp1/pallas_call | solution.py:523
  187.9 3.1 %copy.23 = bf16[256,4096]{1,0:T(8,128)(2,1)} copy(bf16[256,4096]{1,0:T(8,128)(2,1)} %mlp1.1) | data formatting | bytes 4194304

commit v3 on v2

--- a/solution.py
+++ b/solution.py
@@ -26,11 +26,12 @@
 HB = B // 2
 PH = PW // 2
 NC = 23
+UN = True
 
 CB = 32
 NCH = B // CB
-NS = 5
-PF = 3
+NS = 8
+PF = 6
 
 
 def rope_tables(shape):
@@ -89,12 +90,9 @@
         cs = [pltpu.make_async_copy(wq_hbm.at[layer, rs], wq_v.at[rs], wsem.at[c, 0]),
               pltpu.make_async_copy(wk_hbm.at[layer, rs], wk_v.at[rs], wsem.at[c, 1]),
               pltpu.make_async_copy(wv_hbm.at[layer, rs], wv_v.at[rs], wsem.at[c, 2])]
-        for t in cs:
-            t.start()
         wcopies.append(cs)
-    for c in range(PF):
-        for t in kv_in(c, c):
-            t.start()
+    for t in wcopies[0]:
+        t.start()
 
     rid[...] = lax.broadcasted_iota(jnp.int32, (S, HD), 0).astype(F32).astype(BF16)
     cos_t[...], sin_t[...] = rope_tables((S, HD))
@@ -107,7 +105,13 @@
 
     lax.fori_loop(0, B, look_up, 0, unroll=8)
     xcopy.wait()
+    for cs in wcopies[1:]:
+        for t in cs:
+            t.start()
     norm_rows(x_v, h_v, nw_ref, layer)
+    for c in range(PF):
+        for t in kv_in(c, c):
+            t.start()
     for c in range(4):
         for t in wcopies[c]:
             t.wait()
@@ -255,7 +259,7 @@
             pltpu.SemaphoreType.DMA((NS,)),
         ],
         input_output_aliases=alias,
-        compiler_params=pltpu.CompilerParams(vmem_limit_bytes=60 * 2 ** 20),
+        compiler_params=pltpu.CompilerParams(vmem_limit_bytes=40 * 2 ** 20),
     )(*ins)
 
 
@@ -302,9 +306,8 @@
     for i in range(ND):
         rs = pl.ds(i * (FW // ND), FW // ND)
         wds.append(pltpu.make_async_copy(wd_hbm.at[layer, rs], wd_v.at[rs], wsem.at[2 * NG + i]))
-    for t in wos + xcs + gus + wds:
+    for t in wos + xcs:
         t.start()
-    pl.semaphore_wait(barrier, len(peers))
 
     def send(src, dst, i, dev):
         c = pltpu.make_async_remote_copy(src_ref=src, dst_ref=dst, send_sem=ssem.at[i], recv_sem=rsem.at[i],
@@ -312,7 +315,7 @@
         c.start()
         return c
 
-    def reduce_scatter(make):
+    def reduce_scatter(make, enter=False):
         live = [{}, {}]
 
         def pair(h, t):
@@ -333,6 +336,8 @@
             for t, p in enumerate(order):
                 q = other(p)
                 make(h, t, p, q)
+                if enter and (h, t) == (0, 0):
+                    pl.semaphore_wait(barrier, len(peers))
                 live[h]["d%d" % t] = send(part.at[h, q], d2d.at[h, t], NC * h + t, pt)
                 if todo:
                     pair(*todo.pop(0))
@@ -397,12 +402,15 @@
     def out_half(h, i, p, q):
         if h == 0:
             wos[i].wait()
+            if i == 3:
+                for t in gus:
+                    t.start()
         w = jnp.concatenate([wo_v[:, cols(p, h)], wo_v[:, cols(q, h)]], axis=1)
         t = jnp.dot(o_ref[...], w, preferred_element_type=F32).astype(BF16)
         part[h, p] = t[:, :PH]
         part[h, q] = t[:, PH:]
 
-    live = reduce_scatter(out_half)
+    live = reduce_scatter(out_half, True)
     for t in xcs:
         t.wait()
     final(0, live[0])
@@ -424,11 +432,10 @@
         tot = tot + ssb[1 + j]
     rr = lax.rsqrt(tot * (1.0 / D) + 1e-5)
     r_v[...] = jnp.broadcast_to(rr[0:1], (128, B)).T
-    relay(1, live[1])
-    for h in range(2):
-        near(h, live[h])
     for t in gus:
         t.wait()
+    for t in wds:
+        t.start()
 
     TN = 256
 
@@ -462,10 +469,13 @@
                 a_v[:, cs] = (gt * (1.0 / (1.0 + jnp.exp(-gt))) * up).astype(BF16)
             return carry
 
-        lax.fori_loop(0, FW // TN, tile, 0)
+        lax.fori_loop(0, FW // TN, tile, 0, unroll=UN)
 
     got(live, "p0")
     gate_up(me, True, False)
+    relay(1, live[1])
+    for h in range(2):
+        near(h, live[h])
     got(live, "p2", "p3")
     gate_up(xn, False, False)
     for h in range(2):

time: 191 us -> 163 us (0.85)
  Pallas kernels: 187 us -> 145 us
  local copies, waits for them, and re-layouts: 3.13 us -> 16.8 us
    pallas_call x2, Pallas kernels: 145 us -> 115 us  [mlp_call(): pl.pallas_call(functools.partial(mlp_kernel, layer), name=f'mlp{layer}',...]
    unnamed x1 -> x25, local copies, waits for them, and re-layouts: 3.13 us -> 16.8 us
    pallas_call x2, Pallas kernels: 41.9 us -> 29.9 us  [attn_call(): pl.pallas_call(functools.partial(attn_kernel, layer, first), name=f'attn{...]
where the time goes in v3:
time: 163 us
  Pallas kernels  145 us (89%)
  local copies, waits for them, and re-layouts  16.8 us (10%)
    pallas_call x2, Pallas kernels, mlp_call(): pl.pallas_call(functools.partial(mlp_kernel, layer), name=f'mlp{layer}',...  115 us
    pallas_call x2, Pallas kernels, attn_call(): pl.pallas_call(functools.partial(attn_kernel, layer, first), name=f'attn{...  29.9 us
    unnamed x25, local copies, waits for them, and re-layouts  16.8 us

profile of v3, /device:TPU:1, one launch (start us, length us, event | category | flops | bytes accessed | tf_op | source)
XLA Modules:
  0.0 162.5 jit_solution(5680991412340966554)
XLA Ops:
  0.6 0.0 copy-start.1
  0.6 1.6 copy-done.1
  2.2 0.0 copy-start.3
  2.2 1.6 copy-done.3
  3.8 0.0 copy-start.5
  3.8 1.6 copy-done.5
  5.4 0.0 copy-start.8
  5.4 0.7 copy-done.8
  6.1 0.0 copy-start.10
  6.1 0.7 copy-done.10
  6.8 14.9 %attn0.1 = (bf16[256,512]{1,0:T(8,128)(2,1)S(1)}, bf16[2,256,128,128]{3,2,1,0:T(8,128)(2,1)}, bf16[2,256,128,128]{3,2,1,0:T(8,128)(2,1)}) custom-call(s32[256]{0:T(256)S(1)} %copy-done.10, bf16[256,4096]{1,0:T(8,128)(2,1)S(1)} %copy-done.5, bf16[2,4096]{1,0:T(2,128)(2,1)S(1)} %copy-done.8, bf16[2,4096,512]{2,1,0:T(8,128)(2,1)} %wq_hbm.3, ...), custom_call_target="tpu_custom_call" | custom-call | tf_op jit(solution)/shard_map/attn0/pallas_call | solution.py:230
  21.7 0.0 copy-start.7
  21.7 0.7 copy-done.7
  22.4 58.6 %mlp0.1.x_hbm = bf16[256,4096]{1,0:T(8,128)(2,1)} custom-call(bf16[256,512]{1,0:T(8,128)(2,1)} %copy-done.7, bf16[256,4096]{1,0:T(8,128)(2,1)} %x_hbm.3, bf16[2,4096]{1,0:T(2,128)(2,1)} %nw_ref.7, bf16[2,512,4096]{2,1,0:T(8,128)(2,1)} %wo_hbm.3, bf16[2,4096,1792]{2,1,0:T(8,128)(2,1)} %wg_hbm.3, bf16[2,4096,1792]{2,1,0:T(8,128)(2,1)} %wu_hbm.3, ...), custom_call_target="tpu_custom_call" | custom-call | tf_op jit(solution)/shard_map/mlp0/pallas_call | solution.py:533
  80.9 0.0 copy-start
  81.0 1.6 copy-done
  82.5 0.0 copy-start.2
  82.5 1.6 copy-done.2
  84.1 0.0 copy-start.4
  84.1 1.6 copy-done.4
  85.7 0.0 copy-start.9
  85.7 0.7 copy-done.9
  86.4 0.0 copy-start.11
  86.4 0.7 copy-done.11
  87.1 15.1 %attn1.1 = (bf16[256,512]{1,0:T(8,128)(2,1)S(1)}, bf16[2,256,128,128]{3,2,1,0:T(8,128)(2,1)}, bf16[2,256,128,128]{3,2,1,0:T(8,128)(2,1)}) custom-call(s32[256]{0:T(256)S(1)} %copy-done.11, bf16[256,4096]{1,0:T(8,128)(2,1)S(1)} %copy-done, bf16[2,4096]{1,0:T(2,128)(2,1)S(1)} %copy-done.9, ...), custom_call_target="tpu_custom_call", output_to_operand_aliasing={{1}: (8, {}), {2}: (9, {})} | custom-call | tf_op jit(solution)/shard_map/attn1/pallas_call | solution.py:230
  102.2 0.0 copy-start.6
  102.2 0.7 copy-done.6
  102.9 56.5 %mlp1.1 = bf16[256,4096]{1,0:T(8,128)(2,1)} custom-call(bf16[256,512]{1,0:T(8,128)(2,1)} %copy-done.6, bf16[256,4096]{1,0:T(8,128)(2,1)} %mlp0.1.x_hbm, bf16[2,4096]{1,0:T(2,128)(2,1)} %nw_ref.7, bf16[2,512,4096]{2,1,0:T(8,128)(2,1)} %wo_hbm.3, bf16[2,4096,1792]{2,1,0:T(8,128)(2,1)} %wg_hbm.3, bf16[2,4096,1792]{2,1,0:T(8,128)(2,1)} %wu_hbm.3, ...), custom_call_target="tpu_custom_call" | custom-call | tf_op jit(solution)/shard_map/mlp1/pallas_call | solution.py:533
  159.4 3.1 %copy.23 = bf16[256,4096]{1,0:T(8,128)(2,1)} copy(bf16[256,4096]{1,0:T(8,128)(2,1)} %mlp1.1) | data formatting | bytes 4194304
Async XLA Ops:
  0.6 1.6 copy-start.1
  2.2 1.6 copy-start.3
  3.8 1.6 copy-start.5
  5.4 0.7 copy-start.8
  6.1 0.7 copy-start.10
  21.7 0.7 copy-start.7
  80.9 1.6 copy-start
  82.5 1.6 copy-start.2
  84.1 1.6 copy-start.4
  85.7 0.7 copy-start.9
  86.4 0.7 copy-start.11
  102.2 0.7 copy-start.6

commit v4 on v3

--- a/solution.py
+++ b/solution.py
@@ -26,7 +26,6 @@
 HB = B // 2
 PH = PW // 2
 NC = 23
-UN = True
 
 CB = 32
 NCH = B // CB
@@ -259,7 +258,7 @@
             pltpu.SemaphoreType.DMA((NS,)),
         ],
         input_output_aliases=alias,
-        compiler_params=pltpu.CompilerParams(vmem_limit_bytes=40 * 2 ** 20),
+        compiler_params=pltpu.CompilerParams(vmem_limit_bytes=67043328),
     )(*ins)
 
 
@@ -425,6 +424,7 @@
     sss = [send(ssb.at[0], ssb.at[1 + j], 2 * NC + j, d) for j, d in enumerate(peers)]
     gather_start(1, live[1])
     relay(0, live[0])
+    near(0, live[0])
     for t in sss:
         t.wait_recv()
     tot = ssb[0]
@@ -432,6 +432,7 @@
         tot = tot + ssb[1 + j]
     rr = lax.rsqrt(tot * (1.0 / D) + 1e-5)
     r_v[...] = jnp.broadcast_to(rr[0:1], (128, B)).T
+    relay(1, live[1])
     for t in gus:
         t.wait()
     for t in wds:
@@ -439,7 +440,7 @@
 
     TN = 256
 
-    def gate_up(p, first, last):
+    def gate_up(p, first, last, between={}):
         base = pl.multiple_of((p // 2) * 2 * PW, 2 * PW)
 
         def norm_step(i, carry):
@@ -454,9 +455,9 @@
 
         lax.fori_loop(0, B // 64, norm_step, 0)
 
-        def tile(j, carry):
-            cs = pl.ds(pl.multiple_of(j * TN, TN), TN)
-            ks = pl.ds(base, 2 * PW)
+        ks = pl.ds(base, 2 * PW)
+        for j in range(FW // TN):
+            cs = slice(j * TN, (j + 1) * TN)
             w = jnp.concatenate([wg_v[ks, cs], wu_v[ks, cs]], axis=1)
             gu = jnp.dot(hc[...], w, preferred_element_type=F32)
             if not first:
@@ -467,19 +468,13 @@
                 gt = gu[:, :TN].astype(BF16).astype(F32)
                 up = gu[:, TN:].astype(BF16).astype(F32)
                 a_v[:, cs] = (gt * (1.0 / (1.0 + jnp.exp(-gt))) * up).astype(BF16)
-            return carry
-
-        lax.fori_loop(0, FW // TN, tile, 0, unroll=UN)
+            for act, h in between.get(j, ()):
+                act(h, live[h])
 
     got(live, "p0")
-    gate_up(me, True, False)
-    relay(1, live[1])
-    for h in range(2):
-        near(h, live[h])
+    gate_up(me, True, False, {3: [(near, 1)]})
     got(live, "p2", "p3")
-    gate_up(xn, False, False)
-    for h in range(2):
-        far(h, live[h])
+    gate_up(xn, False, False, {2: [(far, 0)], 6: [(far, 1)]})
     got(live, "p1", "p4")
     gate_up(yn, False, False)
     got(live, "p5", "p6")
@@ -562,6 +557,33 @@
     )(o, x, nw, wo, wg, wu, wd)
 
 
+def copy_kernel(x_hbm, o_hbm, buf, isem, osem):
+    n = buf.shape[0]
+    rows = B // n
+    ins = [pltpu.make_async_copy(x_hbm.at[pl.ds(i * rows, rows)], buf.at[i], isem.at[i]) for i in range(n)]
+    outs = [pltpu.make_async_copy(buf.at[i], o_hbm.at[pl.ds(i * rows, rows)], osem.at[i]) for i in range(n)]
+    for t in ins:
+        t.start()
+    for i in range(n):
+        ins[i].wait()
+        outs[i].start()
+    for t in outs:
+        t.wait()
+
+
+def copy_call(x):
+    n = 8
+    return pl.pallas_call(
+        copy_kernel,
+        name="emit",
+        out_shape=jax.ShapeDtypeStruct(x.shape, x.dtype),
+        in_specs=[ANY],
+        out_specs=ANY,
+        scratch_shapes=[pltpu.VMEM((n, B // n, D), BF16), pltpu.SemaphoreType.DMA((n,)), pltpu.SemaphoreType.DMA((n,))],
+        compiler_params=pltpu.CompilerParams(vmem_limit_bytes=67043328),
+    )(x)
+
+
 def solution(mesh):
     row_spec = P('dp', None)
     pos_spec = P('dp')
@@ -579,6 +601,6 @@
             o, ko, vo = attn_call(layer, positions, x, attn_norm, w_query, w_key, w_value, kc, vc, prev)
             prev = (ko, vo)
             x = mlp_call(layer, o, x, mlp_norm, w_out, w_gate, w_up, w_down)
-        return x, prev[0].reshape(k_cache.shape), prev[1].reshape(v_cache.shape)
+        return copy_call(x), prev[0].reshape(k_cache.shape), prev[1].reshape(v_cache.shape)
 
     return jax.shard_map(local_step, mesh=mesh, in_specs=(row_spec, pos_spec, cache_spec, cache_spec, norm_spec, col_spec, col_spec, col_spec, split_rows, norm_spec, col_spec, col_spec, split_rows), out_specs=(row_spec, cache_spec, cache_spec), check_vma=False)

time: 163 us -> 153 us (0.939)
  local copies, waits for them, and re-layouts: 16.8 us -> 0 us
  Pallas kernels: 145 us -> 152 us
    unnamed x25 -> x0, local copies, waits for them, and re-layouts: 16.8 us -> none
    pallas_call x2, Pallas kernels: 29.9 us -> 33.8 us  [attn_call(): pl.pallas_call(functools.partial(attn_kernel, layer, first), name=f'attn{...]
    pallas_call x0 -> x1, Pallas kernels: none -> 2.39 us  [copy_call(): pl.pallas_call(copy_kernel, name='emit', out_shape=jax.ShapeDtypeStruct(x...]
where the time goes in v4:
time: 153 us
  Pallas kernels  152 us (99%)
    pallas_call x2, Pallas kernels, mlp_call(): pl.pallas_call(functools.partial(mlp_kernel, layer), name=f'mlp{layer}',...  116 us
    pallas_call x2, Pallas kernels, attn_call(): pl.pallas_call(functools.partial(attn_kernel, layer, first), name=f'attn{...  33.8 us

profile of v4, /device:TPU:1, one launch (start us, length us, event | category | flops | bytes accessed | tf_op | source)
XLA Modules:
  0.0 152.6 jit_solution(6924228527153263824)
XLA Ops:
  0.6 16.8 %attn0.1 = (bf16[256,512]{1,0:T(8,128)(2,1)}, bf16[2,256,128,128]{3,2,1,0:T(8,128)(2,1)}, bf16[2,256,128,128]{3,2,1,0:T(8,128)(2,1)}) custom-call(s32[256]{0:T(256)} %pos_ref.3, bf16[256,4096]{1,0:T(8,128)(2,1)} %x_hbm.3, bf16[2,4096]{1,0:T(2,128)(2,1)} %nw_ref.6, bf16[2,4096,512]{2,1,0:T(8,128)(2,1)} %wq_hbm.3, bf16[2,4096,128]{2,1,0:T(8,128)(2,1)} %wk_hbm.3, ...), custom_call_target="tpu_custom_call" | custom-call | tf_op jit(solution)/shard_map/attn0/pallas_call | solution.py:229
  17.4 58.6 %mlp0.1.x_hbm = bf16[256,4096]{1,0:T(8,128)(2,1)} custom-call(bf16[256,512]{1,0:T(8,128)(2,1)} %get-tuple-element.9.o_ref, bf16[256,4096]{1,0:T(8,128)(2,1)} %x_hbm.3, bf16[2,4096]{1,0:T(2,128)(2,1)} %nw_ref.7, bf16[2,512,4096]{2,1,0:T(8,128)(2,1)} %wo_hbm.3, bf16[2,4096,1792]{2,1,0:T(8,128)(2,1)} %wg_hbm.3, bf16[2,4096,1792]{2,1,0:T(8,128)(2,1)} %wu_hbm.3, ...), custom_call_target="tpu_custom_call" | custom-call | tf_op jit(solution)/shard_map/mlp0/pallas_call | solution.py:528
  76.0 17.0 %attn1.1 = (bf16[256,512]{1,0:T(8,128)(2,1)}, bf16[2,256,128,128]{3,2,1,0:T(8,128)(2,1)}, bf16[2,256,128,128]{3,2,1,0:T(8,128)(2,1)}) custom-call(s32[256]{0:T(256)} %pos_ref.3, bf16[256,4096]{1,0:T(8,128)(2,1)} %mlp0.1.x_hbm, bf16[2,4096]{1,0:T(2,128)(2,1)} %nw_ref.6, bf16[2,4096,512]{2,1,0:T(8,128)(2,1)} %wq_hbm.3, ...), custom_call_target="tpu_custom_call", output_to_operand_aliasing={{1}: (8, {}), {2}: (9, {})} | custom-call | tf_op jit(solution)/shard_map/attn1/pallas_call | solution.py:229
  93.0 57.0 %mlp1.1.x_hbm = bf16[256,4096]{1,0:T(8,128)(2,1)} custom-call(bf16[256,512]{1,0:T(8,128)(2,1)} %get-tuple-element.12.o_ref, bf16[256,4096]{1,0:T(8,128)(2,1)} %mlp0.1.x_hbm, bf16[2,4096]{1,0:T(2,128)(2,1)} %nw_ref.7, bf16[2,512,4096]{2,1,0:T(8,128)(2,1)} %wo_hbm.3, bf16[2,4096,1792]{2,1,0:T(8,128)(2,1)} %wg_hbm.3, bf16[2,4096,1792]{2,1,0:T(8,128)(2,1)} %wu_hbm.3, ...), custom_call_target="tpu_custom_call" | custom-call | tf_op jit(solution)/shard_map/mlp1/pallas_call | solution.py:528
  150.0 2.4 %emit.1 = bf16[256,4096]{1,0:T(8,128)(2,1)} custom-call(bf16[256,4096]{1,0:T(8,128)(2,1)} %mlp1.1.x_hbm), custom_call_target="tpu_custom_call" | custom-call | tf_op jit(solution)/shard_map/emit/pallas_call | solution.py:576

commit v5 on v4

--- a/solution.py
+++ b/solution.py
@@ -61,14 +61,14 @@
     lax.fori_loop(0, B // rows, step, 0, unroll=2)
 
 
-def attn_kernel(layer, first, pos_ref, x_hbm, nw_ref, wq_hbm, wk_hbm, wv_hbm, kc_hbm, vc_hbm, *rest):
+def attn_kernel(layer, first, pos_hbm, x_hbm, nw_hbm, wq_hbm, wk_hbm, wv_hbm, kc_hbm, vc_hbm, *rest):
     if first:
         o_ref, ko_hbm, vo_hbm = rest[:3]
         rest = rest[3:]
     else:
         o_ref, ko_hbm, vo_hbm = rest[2:5]
         rest = rest[5:]
-    x_v, h_v, cos_t, sin_t, cos_ref, sin_ref, wq_v, wk_v, wv_v, acc, q4, o4, kn, vn, rid, kb, vb, wsem, xsem, ksem, vsem, kosem, vosem = rest
+    pos_ref, nw_ref, x_v, h_v, cos_t, sin_t, cos_ref, sin_ref, wq_v, wk_v, wv_v, acc, qkv_v, q4, o4, kn, vn, rid, kb, vb, wsem, xsem, psem, ksem, vsem, kosem, vosem = rest
 
     def kv_in(c, slot):
         rs = pl.ds(c * CB, CB)
@@ -80,18 +80,28 @@
         return (pltpu.make_async_copy(kb.at[slot], ko_hbm.at[layer, rs], kosem.at[slot]),
                 pltpu.make_async_copy(vb.at[slot], vo_hbm.at[layer, rs], vosem.at[slot]))
 
-    xcopy = pltpu.make_async_copy(x_hbm, x_v, xsem)
-    xcopy.start()
+    poscopy = pltpu.make_async_copy(pos_hbm, pos_ref, psem.at[0])
+    poscopy.start()
     KC = D // 4
-    wcopies = []
-    for c in range(4):
-        rs = pl.ds(c * KC, KC)
-        cs = [pltpu.make_async_copy(wq_hbm.at[layer, rs], wq_v.at[rs], wsem.at[c, 0]),
-              pltpu.make_async_copy(wk_hbm.at[layer, rs], wk_v.at[rs], wsem.at[c, 1]),
-              pltpu.make_async_copy(wv_hbm.at[layer, rs], wv_v.at[rs], wsem.at[c, 2])]
-        wcopies.append(cs)
-    for t in wcopies[0]:
-        t.start()
+    if first:
+        xcopy = pltpu.make_async_copy(x_hbm, x_v, xsem)
+        xcopy.start()
+        nwcopy = pltpu.make_async_copy(nw_hbm, nw_ref, psem.at[1])
+        nwcopy.start()
+        wcopies = []
+        for c in range(4):
+            rs = pl.ds(c * KC, KC)
+            wcopies.append([pltpu.make_async_copy(wq_hbm.at[layer, rs], wq_v.at[rs], wsem.at[c, 0]),
+                            pltpu.make_async_copy(wk_hbm.at[layer, rs], wk_v.at[rs], wsem.at[c, 1]),
+                            pltpu.make_async_copy(wv_hbm.at[layer, rs], wv_v.at[rs], wsem.at[c, 2])])
+        for t in wcopies[0]:
+            t.start()
+    else:
+        xcopy = pltpu.make_async_copy(x_hbm, qkv_v, xsem)
+        xcopy.start()
+        for c in range(PF):
+            for t in kv_in(c, c):
+                t.start()
 
     rid[...] = lax.broadcasted_iota(jnp.int32, (S, HD), 0).astype(F32).astype(BF16)
     cos_t[...], sin_t[...] = rope_tables((S, HD))
@@ -102,25 +112,31 @@
         sin_ref[pl.ds(b, 1), :] = sin_t[pl.ds(p, 1), :]
         return carry
 
+    poscopy.wait()
     lax.fori_loop(0, B, look_up, 0, unroll=8)
     xcopy.wait()
-    for cs in wcopies[1:]:
-        for t in cs:
-            t.start()
-    norm_rows(x_v, h_v, nw_ref, layer)
-    for c in range(PF):
-        for t in kv_in(c, c):
-            t.start()
-    for c in range(4):
-        for t in wcopies[c]:
-            t.wait()
-        rs = slice(c * KC, (c + 1) * KC)
-        w = jnp.concatenate([wq_v[rs, :], wk_v[rs, :], wv_v[rs, :]], axis=1)
-        r = jnp.dot(h_v[:, rs], w, preferred_element_type=F32)
-        if c == 0:
-            acc[...] = r
-        else:
-            acc[...] += r
+    if first:
+        nwcopy.wait()
+        for cs in wcopies[1:]:
+            for t in cs:
+                t.start()
+        norm_rows(x_v, h_v, nw_ref, layer)
+        for c in range(PF):
+            for t in kv_in(c, c):
+                t.start()
+        for c in range(4):
+            for t in wcopies[c]:
+                t.wait()
+            rs = slice(c * KC, (c + 1) * KC)
+            w = jnp.concatenate([wq_v[rs, :], wk_v[rs, :], wv_v[rs, :]], axis=1)
+            r = jnp.dot(h_v[:, rs], w, preferred_element_type=F32)
+            if c == 0:
+                acc[...] = r
+            else:
+                acc[...] += r
+        qkv = acc
+    else:
+        qkv = qkv_v
 
     cos = cos_ref[...]
     sin = sin_ref[...]
@@ -130,9 +146,9 @@
         return (t * cos + pltpu.roll(t, HD // 2, 1) * sin).astype(BF16).astype(F32)
 
     for hd in range(G):
-        q4[pl.ds(hd, B, stride=G), :] = rope(acc[:, hd * HD:(hd + 1) * HD])
-    kn[...] = rope(acc[:, QW:QW + HD])
-    vn[...] = acc[:, QW + HD:QW + 2 * HD].astype(BF16).astype(F32)
+        q4[pl.ds(hd, B, stride=G), :] = rope(qkv[:, hd * HD:(hd + 1) * HD])
+    kn[...] = rope(qkv[:, QW:QW + HD])
+    vn[...] = qkv[:, QW + HD:QW + 2 * HD].astype(BF16).astype(F32)
 
     scale = HD ** -0.5
     row = lax.broadcasted_iota(jnp.int32, (4 * G, HD), 0) // G
@@ -220,7 +236,7 @@
     first = prev is None
     cache = jax.ShapeDtypeStruct(kc.shape, BF16)
     ins = [pos, x, nw, wq, wk, wv, kc, vc]
-    specs = [SMEM, ANY, VMEM] + [ANY] * 5
+    specs = [ANY] * 8
     alias = {}
     if not first:
         alias = {len(ins): 1, len(ins) + 1: 2}
@@ -233,6 +249,8 @@
         in_specs=specs,
         out_specs=(VMEM, ANY, ANY),
         scratch_shapes=[
+            pltpu.SMEM((B,), jnp.int32),
+            pltpu.VMEM((2, D), BF16),
             pltpu.VMEM((B, D), BF16),
             pltpu.VMEM((B, D), BF16),
             pltpu.VMEM((S, HD), F32),
@@ -243,6 +261,7 @@
             pltpu.VMEM((D, HD), BF16),
             pltpu.VMEM((D, HD), BF16),
             pltpu.VMEM((B, QW + 2 * HD), F32),
+            pltpu.VMEM((B, QW + 2 * HD), BF16),
             pltpu.VMEM((B * G, HD), F32),
             pltpu.VMEM((B * G, HD), F32),
             pltpu.VMEM((B, HD), F32),
@@ -252,6 +271,7 @@
             pltpu.VMEM((NS, CB, S, HD), BF16),
             pltpu.SemaphoreType.DMA((4, 3)),
             pltpu.SemaphoreType.DMA,
+            pltpu.SemaphoreType.DMA((2,)),
             pltpu.SemaphoreType.DMA((NS,)),
             pltpu.SemaphoreType.DMA((NS,)),
             pltpu.SemaphoreType.DMA((NS,)),
@@ -262,9 +282,15 @@
     )(*ins)
 
 
-def mlp_kernel(layer, o_ref, x_hbm, nw_ref, wo_hbm, wg_hbm, wu_hbm, wd_hbm, xo_hbm,
-               wo_v, wg_v, wu_v, wd_v, part, xg, hc, acc, a_v, xown, d2d, r1, r2, ssb, r_v,
-               wsem, osem, xsem, ssem, rsem):
+def mlp_kernel(layer, last, o_hbm, x_hbm, nw_hbm, an_hbm, wo_hbm, wg_hbm, wu_hbm, wd_hbm, wq_hbm, wk_hbm, wv_hbm, *rest):
+    if last:
+        xo_hbm = rest[0]
+        rest = rest[1:]
+    else:
+        xo_hbm, qkv_hbm = rest[:2]
+        rest = rest[2:]
+    (o_ref, nw_ref, an_ref, wo_v, wg_v, wu_v, wd_v, part, xg, hc, acc, a_v, qkv_v, xown, d2d, r1, r2, ssb, r_v,
+     wsem, osem, xsem, isem, qsem, ssem, rsem) = rest
     me = lax.axis_index("tp")
     k = me % 2
     cx = (me // 2) % 2
@@ -293,7 +319,7 @@
         pl.semaphore_signal(barrier, inc=1, device_id={"tp": d}, device_id_type=MESH)
 
     wos = [pltpu.make_async_copy(wo_hbm.at[layer, :, chip_cols(p)], wo_v.at[:, chip_cols(p)], osem.at[i]) for i, p in enumerate(order)]
-    xcs = [pltpu.make_async_copy(x_hbm.at[:, cols(me, h)], xown.at[h], xsem.at[h]) for h in range(2)]
+    xcs = [pltpu.make_async_copy(x_hbm.at[h] if last else x_hbm.at[:, cols(me, h)], xown.at[h], xsem.at[h]) for h in range(2)]
     NG = 4
     gus = []
     for i in range(NG):
@@ -305,8 +331,11 @@
     for i in range(ND):
         rs = pl.ds(i * (FW // ND), FW // ND)
         wds.append(pltpu.make_async_copy(wd_hbm.at[layer, rs], wd_v.at[rs], wsem.at[2 * NG + i]))
-    for t in wos + xcs:
+    ocopy = pltpu.make_async_copy(o_hbm, o_ref, isem.at[0])
+    ncopies = [pltpu.make_async_copy(nw_hbm, nw_ref, isem.at[1]), pltpu.make_async_copy(an_hbm, an_ref, isem.at[2])]
+    for t in [ocopy] + wos + ncopies + xcs:
         t.start()
+    ocopy.wait()
 
     def send(src, dst, i, dev):
         c = pltpu.make_async_remote_copy(src_ref=src, dst_ref=dst, send_sem=ssem.at[i], recv_sem=rsem.at[i],
@@ -409,38 +438,25 @@
         part[h, p] = t[:, :PH]
         part[h, q] = t[:, PH:]
 
-    live = reduce_scatter(out_half, True)
-    for t in xcs:
-        t.wait()
-    final(0, live[0])
-    gather_start(0, live[0])
-    final(1, live[1])
-    sq = jnp.zeros((B, 128), F32)
-    for h in range(2):
-        for c in range(PH // 128):
-            t = xg[h, me, :, c * 128:(c + 1) * 128].astype(F32)
-            sq = sq + t * t
-    ssb[0] = jnp.broadcast_to(jnp.sum(sq.T, axis=0, keepdims=True), (8, B))
-    sss = [send(ssb.at[0], ssb.at[1 + j], 2 * NC + j, d) for j, d in enumerate(peers)]
-    gather_start(1, live[1])
-    relay(0, live[0])
-    near(0, live[0])
-    for t in sss:
-        t.wait_recv()
-    tot = ssb[0]
-    for j in range(len(peers)):
-        tot = tot + ssb[1 + j]
-    rr = lax.rsqrt(tot * (1.0 / D) + 1e-5)
-    r_v[...] = jnp.broadcast_to(rr[0:1], (128, B)).T
-    relay(1, live[1])
-    for t in gus:
-        t.wait()
-    for t in wds:
-        t.start()
-
-    TN = 256
-
-    def gate_up(p, first, last, between={}):
+    def square_start():
+        sq = jnp.zeros((B, 128), F32)
+        for h in range(2):
+            for c in range(PH // 128):
+                t = xg[h, me, :, c * 128:(c + 1) * 128].astype(F32)
+                sq = sq + t * t
+        ssb[0] = jnp.broadcast_to(jnp.sum(sq.T, axis=0, keepdims=True), (8, B))
+        return [send(ssb.at[0], ssb.at[1 + j], 2 * NC + j, d) for j, d in enumerate(peers)]
+
+    def square_end(sss):
+        for t in sss:
+            t.wait_recv()
+        tot = ssb[0]
+        for j in range(len(peers)):
+            tot = tot + ssb[1 + j]
+        rr = lax.rsqrt(tot * (1.0 / D) + 1e-5)
+        r_v[...] = jnp.broadcast_to(rr[0:1], (128, B)).T
+
+    def norm_chunk(p, w_ref, row):
         base = pl.multiple_of((p // 2) * 2 * PW, 2 * PW)
 
         def norm_step(i, carry):
@@ -449,13 +465,34 @@
             for c in range(2 * PW // 128):
                 cs = slice(c * 128, (c + 1) * 128)
                 e, h, o = c // 4, (c // 2) % 2, (c % 2) * 128
-                w = nw_ref[layer:layer + 1, pl.ds(pl.multiple_of(base + c * 128, 128), 128)].astype(F32)
+                w = w_ref[row:row + 1, pl.ds(pl.multiple_of(base + c * 128, 128), 128)].astype(F32)
                 hc[sl, cs] = (xg[h, (p // 2) * 2 + e, sl, o:o + 128].astype(F32) * r * w).astype(BF16)
             return carry
 
         lax.fori_loop(0, B // 64, norm_step, 0)
-
-        ks = pl.ds(base, 2 * PW)
+        return pl.ds(base, 2 * PW)
+
+    live = reduce_scatter(out_half, True)
+    for t in xcs + ncopies:
+        t.wait()
+    final(0, live[0])
+    gather_start(0, live[0])
+    final(1, live[1])
+    sss = square_start()
+    gather_start(1, live[1])
+    relay(0, live[0])
+    near(0, live[0])
+    square_end(sss)
+    relay(1, live[1])
+    for t in gus:
+        t.wait()
+    for t in wds:
+        t.start()
+
+    TN = 256
+
+    def gate_up(p, first, last, between={}):
+        ks = norm_chunk(p, nw_ref, layer)
         for j in range(FW // TN):
             cs = slice(j * TN, (j + 1) * TN)
             w = jnp.concatenate([wg_v[ks, cs], wu_v[ks, cs]], axis=1)
@@ -482,8 +519,18 @@
     drain(live)
     for t in sss:
         t.wait_send()
+    if not last:
+        qs = []
+        for i in range(2):
+            rs = pl.ds(i * (D // 2), D // 2)
+            qs += [pltpu.make_async_copy(wq_hbm.at[layer + 1, rs], wg_v.at[rs, pl.ds(0, QW)], qsem.at[i, 0]),
+                   pltpu.make_async_copy(wk_hbm.at[layer + 1, rs], wg_v.at[rs, pl.ds(QW, HD)], qsem.at[i, 1]),
+                   pltpu.make_async_copy(wv_hbm.at[layer + 1, rs], wg_v.at[rs, pl.ds(QW + HD, HD)], qsem.at[i, 2])]
     for t in wds:
         t.wait()
+    if not last:
+        for t in qs:
+            t.start()
 
     def down_half(h, i, p, q):
         w = jnp.concatenate([wd_v[:, cols(p, h)], wd_v[:, cols(q, h)]], axis=1)
@@ -492,46 +539,100 @@
         part[h, q] = t[:, PH:]
 
     live = reduce_scatter(down_half)
-    for h in range(2):
-        final(h, live[h])
-        gather_start(h, live[h])
-    for h in range(2):
-        relay(h, live[h])
-    for h in range(2):
-        near(h, live[h])
-    outs = []
-
-    def write(p):
-        for e in range(2):
-            for h in range(2):
-                n = (p // 2) * 2 + e
-                c = pltpu.make_async_copy(xg.at[h, n], xo_hbm.at[:, cols(n, h)], wsem.at[len(outs)])
-                c.start()
-                outs.append(c)
-
-    got(live, "p0")
-    write(me)
-    for h in range(2):
-        far(h, live[h])
-    got(live, "p2", "p3")
-    write(xn)
-    got(live, "p1", "p4")
-    write(yn)
-    got(live, "p5", "p6")
-    write(dg)
-    drain(live)
-    for c in outs:
-        c.wait()
-
-
-def mlp_call(layer, o, x, nw, wo, wg, wu, wd):
+    if last:
+        for h in range(2):
+            final(h, live[h])
+            gather_start(h, live[h])
+        for h in range(2):
+            relay(h, live[h])
+        for h in range(2):
+            near(h, live[h])
+        outs = []
+
+        def write(p):
+            for e in range(2):
+                for h in range(2):
+                    n = (p // 2) * 2 + e
+                    c = pltpu.make_async_copy(xg.at[h, n], xo_hbm.at[:, cols(n, h)], wsem.at[len(outs)])
+                    c.start()
+                    outs.append(c)
+
+        got(live, "p0")
+        write(me)
+        for h in range(2):
+            far(h, live[h])
+        got(live, "p2", "p3")
+        write(xn)
+        got(live, "p1", "p4")
+        write(yn)
+        got(live, "p5", "p6")
+        write(dg)
+        drain(live)
+        for c in outs:
+            c.wait()
+    else:
+        final(0, live[0])
+        gather_start(0, live[0])
+        final(1, live[1])
+        sss = square_start()
+        gather_start(1, live[1])
+        outs = [pltpu.make_async_copy(xown, xo_hbm, isem.at[0])]
+        outs[0].start()
+        relay(0, live[0])
+        near(0, live[0])
+        square_end(sss)
+        relay(1, live[1])
+        near(1, live[1])
+        for t in qs:
+            t.wait()
+
+        def qkv(p, first, end):
+            ks = norm_chunk(p, an_ref, layer + 1)
+            r = jnp.dot(hc[...], wg_v[ks, :QW + 2 * HD], preferred_element_type=F32)
+            if not first:
+                r = r + jnp.concatenate([acc[0], acc[1, :, :2 * HD]], axis=1)
+            if end:
+                qkv_v[...] = r.astype(BF16)
+            else:
+                acc[0] = r[:, :QW]
+                acc[1, :, :2 * HD] = r[:, QW:]
+
+        got(live, "p0")
+        qkv(me, True, False)
+        far(0, live[0])
+        got(live, "p2", "p3")
+        qkv(xn, False, False)
+        far(1, live[1])
+        got(live, "p1", "p4")
+        qkv(yn, False, False)
+        got(live, "p5", "p6")
+        qkv(dg, False, True)
+        outs.append(pltpu.make_async_copy(qkv_v, qkv_hbm, isem.at[1]))
+        outs[1].start()
+        drain(live)
+        for t in sss:
+            t.wait_send()
+        for c in outs:
+            c.wait()
+
+
+def mlp_call(layer, last, o, x, nw, an, wo, wg, wu, wd, wq, wk, wv):
+    if last:
+        out_shape = jax.ShapeDtypeStruct((B, D), BF16)
+        out_specs = ANY
+    else:
+        out_shape = (jax.ShapeDtypeStruct((2, B, PH), BF16), jax.ShapeDtypeStruct((B, QW + 2 * HD), BF16))
+        out_specs = (ANY, ANY)
     return pl.pallas_call(
-        functools.partial(mlp_kernel, layer),
+        functools.partial(mlp_kernel, layer, last),
         name=f"mlp{layer}",
-        out_shape=jax.ShapeDtypeStruct((B, D), BF16),
-        in_specs=[VMEM, ANY, VMEM, ANY, ANY, ANY, ANY],
-        out_specs=ANY,
+        out_shape=out_shape,
+        in_specs=[ANY] * 11,
+        out_specs=out_specs,
         scratch_shapes=[
+            pltpu.VMEM((B, QW), BF16),
+            pltpu.VMEM((2, D), BF16),
+            pltpu.VMEM((2, D), BF16),
             pltpu.VMEM((QW, D), BF16),
             pltpu.VMEM((D, FW), BF16),
             pltpu.VMEM((D, FW), BF16),
@@ -541,6 +642,7 @@
             pltpu.VMEM((B, 2 * PW), BF16),
             pltpu.VMEM((FW // 256, B, 512), F32),
             pltpu.VMEM((B, FW), BF16),
+            pltpu.VMEM((B, QW + 2 * HD), BF16),
             pltpu.VMEM((2, B, PH), BF16),
             pltpu.VMEM((2, 4, B, PH), BF16),
             pltpu.VMEM((2, 4, HB, PH), BF16),
@@ -550,11 +652,13 @@
             pltpu.SemaphoreType.DMA((16,)),
             pltpu.SemaphoreType.DMA((4,)),
             pltpu.SemaphoreType.DMA((2,)),
+            pltpu.SemaphoreType.DMA((3,)),
+            pltpu.SemaphoreType.DMA((2, 3)),
             pltpu.SemaphoreType.DMA((2 * NC + 7,)),
             pltpu.SemaphoreType.DMA((2 * NC + 7,)),
         ],
         compiler_params=pltpu.CompilerParams(collective_id=layer, has_side_effects=True, vmem_limit_bytes=67043328),
-    )(o, x, nw, wo, wg, wu, wd)
+    )(o, x, nw, an, wo, wg, wu, wd, wq, wk, wv)
 
 
 def copy_kernel(x_hbm, o_hbm, buf, isem, osem):
@@ -598,9 +702,13 @@
         x = hidden
         prev = None
         for layer in range(2):
-            o, ko, vo = attn_call(layer, positions, x, attn_norm, w_query, w_key, w_value, kc, vc, prev)
+            o, ko, vo = attn_call(layer, positions, x if layer == 0 else qkv, attn_norm, w_query, w_key, w_value, kc, vc, prev)
             prev = (ko, vo)
-            x = mlp_call(layer, o, x, mlp_norm, w_out, w_gate, w_up, w_down)
+            y = mlp_call(layer, layer == 1, o, x, mlp_norm, attn_norm, w_out, w_gate, w_up, w_down, w_query, w_key, w_value)
+            if layer == 0:
+                x, qkv = y
+            else:
+                x = y
         return copy_call(x), prev[0].reshape(k_cache.shape), prev[1].reshape(v_cache.shape)
 
     return jax.shard_map(local_step, mesh=mesh, in_specs=(row_spec, pos_spec, cache_spec, cache_spec, norm_spec, col_spec, col_spec, col_spec, split_rows, norm_spec, col_spec, col_spec, split_rows), out_specs=(row_spec, cache_spec, cache_spec), check_vma=False)

time: 153 us -> 150 us (0.980)
  Pallas kernels: 152 us -> 149 us
    pallas_call x2, Pallas kernels: 33.8 us -> 30.7 us  [attn_call(): pl.pallas_call(functools.partial(attn_kernel, layer, first), name=f'attn{...]
where the time goes in v5:
time: 150 us
  Pallas kernels  149 us (99%)
    pallas_call x2, Pallas kernels, mlp_call(): pl.pallas_call(functools.partial(mlp_kernel, layer, last), name=f'mlp{lay...  116 us
    pallas_call x2, Pallas kernels, attn_call(): pl.pallas_call(functools.partial(attn_kernel, layer, first), name=f'attn{...  30.7 us

profile of v5, /device:TPU:1, one launch (start us, length us, event | category | flops | bytes accessed | tf_op | source)
XLA Modules:
  0.0 149.7 jit_solution(503848765317675009)
XLA Ops:
  0.6 16.1 %attn0.1 = (bf16[256,512]{1,0:T(8,128)(2,1)}, bf16[2,256,128,128]{3,2,1,0:T(8,128)(2,1)}, bf16[2,256,128,128]{3,2,1,0:T(8,128)(2,1)}) custom-call(s32[256]{0:T(256)} %pos_hbm.3, bf16[256,4096]{1,0:T(8,128)(2,1)} %x_hbm.3, bf16[2,4096]{1,0:T(2,128)(2,1)} %an_hbm.3, bf16[2,4096,512]{2,1,0:T(8,128)(2,1)} %wq_hbm.7, bf16[2,4096,128]{2,1,0:T(8,128)(2,1)} %wk_hbm.7, ...), custom_call_target="tpu_custom_call" | custom-call | tf_op jit(solution)/shard_map/attn0/pallas_call | solution.py:245
  16.7 59.7 %mlp0.1 = (bf16[2,256,256]{2,1,0:T(8,128)(2,1)}, bf16[256,768]{1,0:T(8,128)(2,1)}) custom-call(bf16[256,512]{1,0:T(8,128)(2,1)} %get-tuple-element.11.o_hbm, bf16[256,4096]{1,0:T(8,128)(2,1)} %x_hbm.3, bf16[2,4096]{1,0:T(2,128)(2,1)} %nw_hbm.7, bf16[2,4096]{1,0:T(2,128)(2,1)} %an_hbm.3, bf16[2,512,4096]{2,1,0:T(8,128)(2,1)} %wo_hbm.3, ...), custom_call_target="tpu_custom_call" | custom-call | tf_op jit(solution)/shard_map/mlp0/pallas_call | solution.py:626
  76.4 14.6 %attn1.1 = (bf16[256,512]{1,0:T(8,128)(2,1)}, bf16[2,256,128,128]{3,2,1,0:T(8,128)(2,1)}, bf16[2,256,128,128]{3,2,1,0:T(8,128)(2,1)}) custom-call(s32[256]{0:T(256)} %pos_hbm.3, bf16[256,768]{1,0:T(8,128)(2,1)} %get-tuple-element.12.x_hbm, bf16[2,4096]{1,0:T(2,128)(2,1)} %an_hbm.3, ...), custom_call_target="tpu_custom_call", output_to_operand_aliasing={{1}: (8, {}), {2}: (9, {})} | custom-call | tf_op jit(solution)/shard_map/attn1/pallas_call | solution.py:245
  91.0 56.1 %mlp1.1.x_hbm = bf16[256,4096]{1,0:T(8,128)(2,1)} custom-call(bf16[256,512]{1,0:T(8,128)(2,1)} %get-tuple-element.15.o_hbm, bf16[2,256,256]{2,1,0:T(8,128)(2,1)} %get-tuple-element.16.x_hbm, bf16[2,4096]{1,0:T(2,128)(2,1)} %nw_hbm.7, bf16[2,4096]{1,0:T(2,128)(2,1)} %an_hbm.3, bf16[2,512,4096]{2,1,0:T(8,128)(2,1)} %wo_hbm.3, bf16[2,4096,1792]{2,1,0:T(8,128)(2,1)} %wg_hbm.3, ...), custom_call_target="tpu_custom_call" | custom-call | tf_op jit(solution)/shard_map/mlp1/pallas_call | solution.py:626
  147.1 2.4 %emit.1 = bf16[256,4096]{1,0:T(8,128)(2,1)} custom-call(bf16[256,4096]{1,0:T(8,128)(2,1)} %mlp1.1.x_hbm), custom_call_target="tpu_custom_call" | custom-call | tf_op jit(solution)/shard_map/emit/pallas_call | solution.py:680

commit v6 on v5

--- a/solution.py
+++ b/solution.py
@@ -68,7 +68,7 @@
     else:
         o_ref, ko_hbm, vo_hbm = rest[2:5]
         rest = rest[5:]
-    pos_ref, nw_ref, x_v, h_v, cos_t, sin_t, cos_ref, sin_ref, wq_v, wk_v, wv_v, acc, qkv_v, q4, o4, kn, vn, rid, kb, vb, wsem, xsem, psem, ksem, vsem, kosem, vosem = rest
+    pos_ref, nw_ref, x_v, h_v, cos_t, sin_t, cos_ref, sin_ref, wq_v, wk_v, wv_v, acc, qkv_v, o_v, q4, o4, kn, vn, rid, kb, vb, wsem, xsem, psem, ksem, vsem, kosem, vosem = rest
 
     def kv_in(c, slot):
         rs = pl.ds(c * CB, CB)
@@ -169,7 +169,6 @@
     def scores(c):
         slot = c % NS
         b0 = c * CB
-        kv_in(c, slot)[0].wait()
         rowid = rid[...]
         out = []
         for g in range(CB // 4):
@@ -183,7 +182,6 @@
     def values(c, s):
         slot = c % NS
         b0 = c * CB
-        kv_in(c, slot)[1].wait()
         rowid = rid[...]
         posr = []
         for g in range(CB // 4):
@@ -212,10 +210,16 @@
                 kv_out(nxt - NS, nxt % NS)[j].wait()
             kv_in(nxt, nxt % NS)[j].start()
 
+    def arrived(c, j):
+        kv_in(c, c % NS)[j].wait()
+
+    arrived(0, 0)
     s0 = scores(0)
     turn(0, 0)
 
     def chunk(c, s):
+        arrived(c + 1, 0)
+        arrived(c, 1)
         sn = scores(c + 1)
         values(c, s)
         turn(c + 1, 0)
@@ -223,13 +227,17 @@
         return sn
 
     sl = lax.fori_loop(0, NCH - 1, chunk, s0)
+    arrived(NCH - 1, 1)
     values(NCH - 1, sl)
     turn(NCH - 1, 1)
     for hd in range(G):
-        o_ref[:, hd * HD:(hd + 1) * HD] = o4[pl.ds(hd, B, stride=G), :].astype(BF16)
+        o_v[:, hd * HD:(hd + 1) * HD] = o4[pl.ds(hd, B, stride=G), :].astype(BF16)
+    ocopy = pltpu.make_async_copy(o_v, o_ref, xsem)
+    ocopy.start()
     for c in range(NCH - NS, NCH):
         for t in kv_out(c, c % NS):
             t.wait()
+    ocopy.wait()
 
 
 def attn_call(layer, pos, x, nw, wq, wk, wv, kc, vc, prev):
@@ -247,7 +255,7 @@
         name=f"attn{layer}",
         out_shape=(jax.ShapeDtypeStruct((B, QW), BF16), cache, cache),
         in_specs=specs,
-        out_specs=(VMEM, ANY, ANY),
+        out_specs=(ANY, ANY, ANY),
         scratch_shapes=[
             pltpu.SMEM((B,), jnp.int32),
             pltpu.VMEM((2, D), BF16),
@@ -262,6 +270,7 @@
             pltpu.VMEM((D, HD), BF16),
             pltpu.VMEM((B, QW + 2 * HD), F32),
             pltpu.VMEM((B, QW + 2 * HD), BF16),
+            pltpu.VMEM((B, QW), BF16),
             pltpu.VMEM((B * G, HD), F32),
             pltpu.VMEM((B * G, HD), F32),
             pltpu.VMEM((B, HD), F32),
@@ -337,9 +346,12 @@
         t.start()
     ocopy.wait()
 
+    def remote(src, dst, i, dev):
+        return pltpu.make_async_remote_copy(src_ref=src, dst_ref=dst, send_sem=ssem.at[i], recv_sem=rsem.at[i],
+                                            device_id={"tp": dev}, device_id_type=MESH)
+
     def send(src, dst, i, dev):
-        c = pltpu.make_async_remote_copy(src_ref=src, dst_ref=dst, send_sem=ssem.at[i], recv_sem=rsem.at[i],
-                                         device_id={"tp": dev}, device_id_type=MESH)
+        c = remote(src, dst, i, dev)
         c.start()
         return c
 
@@ -390,14 +402,17 @@
             xown[h, rs] = new
             xg[h, me, rs] = new
 
-    def gather_start(h, c):
-        def go(name, p, rs, i, dev):
-            c[name] = send(xg.at[h, p, rs], xg.at[h, p, rs], NC * h + i, dev)
-        go("ga0", me, top, 10, yn)
-        go("gb0", me, bot, 11, xn)
-        go("ga1", me, top, 12, xn)
-        go("gb1", me, bot, 13, yn)
+    def go(h, c, name, p, rs, i, dev):
+        c[name] = send(xg.at[h, p, rs], xg.at[h, p, rs], NC * h + i, dev)
+
+    def gather_first(h, c):
+        go(h, c, "ga0", me, top, 10, yn)
+        go(h, c, "gb0", me, bot, 11, xn)
         c["p0"] = send(xg.at[h, me], xg.at[h, me], NC * h + 14, pt)
+
+    def gather_second(h, c):
+        go(h, c, "ga1", me, top, 12, xn)
+        go(h, c, "gb1", me, bot, 13, yn)
 
     def forward(h, c, got, name, p, rs, i):
         c[got].wait_recv()
@@ -456,11 +471,11 @@
         rr = lax.rsqrt(tot * (1.0 / D) + 1e-5)
         r_v[...] = jnp.broadcast_to(rr[0:1], (128, B)).T
 
-    def norm_chunk(p, w_ref, row):
+    def norm_rows_of(p, w_ref, row, first, n):
         base = pl.multiple_of((p // 2) * 2 * PW, 2 * PW)
 
         def norm_step(i, carry):
-            sl = pl.ds(pl.multiple_of(i * 64, 64), 64)
+            sl = pl.ds(pl.multiple_of(first + i * 64, 64), 64)
             r = r_v[sl, :]
             for c in range(2 * PW // 128):
                 cs = slice(c * 128, (c + 1) * 128)
@@ -469,19 +484,31 @@
                 hc[sl, cs] = (xg[h, (p // 2) * 2 + e, sl, o:o + 128].astype(F32) * r * w).astype(BF16)
             return carry
 
-        lax.fori_loop(0, B // 64, norm_step, 0)
+        lax.fori_loop(0, n // 64, norm_step, 0)
         return pl.ds(base, 2 * PW)
+
+    def norm_chunk(ps, w_ref, row):
+        if len(ps) == 1:
+            return [norm_rows_of(ps[0], w_ref, row, 0, B)]
+        return [norm_rows_of(p, w_ref, row, i * HB, HB) for i, p in enumerate(ps)]
+
+    def chunk_dot(kss, weight):
+        if len(kss) == 1:
+            return jnp.dot(hc[...], weight(kss[0]), preferred_element_type=F32)
+        return jnp.concatenate([jnp.dot(hc[i * HB:(i + 1) * HB, :], weight(ks), preferred_element_type=F32)
+                                for i, ks in enumerate(kss)], axis=0)
 
     live = reduce_scatter(out_half, True)
     for t in xcs + ncopies:
         t.wait()
     final(0, live[0])
-    gather_start(0, live[0])
+    gather_first(0, live[0])
     final(1, live[1])
     sss = square_start()
-    gather_start(1, live[1])
+    gather_first(1, live[1])
+    for h in range(2):
+        gather_second(h, live[h])
     relay(0, live[0])
-    near(0, live[0])
     square_end(sss)
     relay(1, live[1])
     for t in gus:
@@ -491,12 +518,11 @@
 
     TN = 256
 
-    def gate_up(p, first, last, between={}):
-        ks = norm_chunk(p, nw_ref, layer)
+    def gate_up(ps, first, last, between={}):
+        kss = norm_chunk(ps, nw_ref, layer)
         for j in range(FW // TN):
             cs = slice(j * TN, (j + 1) * TN)
-            w = jnp.concatenate([wg_v[ks, cs], wu_v[ks, cs]], axis=1)
-            gu = jnp.dot(hc[...], w, preferred_element_type=F32)
+            gu = chunk_dot(kss, lambda ks: jnp.concatenate([wg_v[ks, cs], wu_v[ks, cs]], axis=1))
             if not first:
                 gu = gu + acc[j]
             if not last:
@@ -505,17 +531,31 @@
                 gt = gu[:, :TN].astype(BF16).astype(F32)
                 up = gu[:, TN:].astype(BF16).astype(F32)
                 a_v[:, cs] = (gt * (1.0 / (1.0 + jnp.exp(-gt))) * up).astype(BF16)
-            for act, h in between.get(j, ()):
-                act(h, live[h])
+            if j in between:
+                between[j]()
 
     got(live, "p0")
-    gate_up(me, True, False, {3: [(near, 1)]})
-    got(live, "p2", "p3")
-    gate_up(xn, False, False, {2: [(far, 0)], 6: [(far, 1)]})
-    got(live, "p1", "p4")
-    gate_up(yn, False, False)
+    gate_up([me], True, False)
+    near(0, live[0])
+
+    def crossed(i, carry):
+        for h in range(2):
+            for n in (15 + 4 * i, 17 + 3 * i):
+                remote(xg.at[h, me, top], xg.at[h, me, top], NC * h + n, pt).wait_recv()
+
+        def sends():
+            pl.when(i == 0)(lambda: near(1, dict(live[1])))
+            pl.when(i == 1)(lambda: far(0, dict(live[0])))
+
+        gate_up([yn + i * (xn - yn), xn + i * (yn - xn)], False, False, {2: sends})
+        return carry
+
+    lax.fori_loop(0, 2, crossed, 0)
+    for h, name, p, rs, i in ((1, "p3", xn, top, 19), (1, "p4", yn, bot, 20), (0, "p5", dg, top, 21), (0, "p6", dg, bot, 22)):
+        live[h][name] = remote(xg.at[h, p, rs], xg.at[h, p, rs], NC * h + i, pt)
+    far(1, live[1])
     got(live, "p5", "p6")
-    gate_up(dg, False, True)
+    gate_up([dg], False, True)
     drain(live)
     for t in sss:
         t.wait_send()
@@ -542,7 +582,9 @@
     if last:
         for h in range(2):
             final(h, live[h])
-            gather_start(h, live[h])
+            gather_first(h, live[h])
+        for h in range(2):
+            gather_second(h, live[h])
         for h in range(2):
             relay(h, live[h])
         for h in range(2):
@@ -572,23 +614,25 @@
             c.wait()
     else:
         final(0, live[0])
-        gather_start(0, live[0])
+        gather_first(0, live[0])
         final(1, live[1])
         sss = square_start()
-        gather_start(1, live[1])
+        gather_first(1, live[1])
+        for h in range(2):
+            gather_second(h, live[h])
         outs = [pltpu.make_async_copy(xown, xo_hbm, isem.at[0])]
         outs[0].start()
         relay(0, live[0])
-        near(0, live[0])
         square_end(sss)
         relay(1, live[1])
-        near(1, live[1])
+        for h in range(2):
+            near(h, live[h])
         for t in qs:
             t.wait()
 
-        def qkv(p, first, end):
-            ks = norm_chunk(p, an_ref, layer + 1)
-            r = jnp.dot(hc[...], wg_v[ks, :QW + 2 * HD], preferred_element_type=F32)
+        def qkv(ps, first, end):
+            kss = norm_chunk(ps, an_ref, layer + 1)
+            r = chunk_dot(kss, lambda ks: wg_v[ks, :QW + 2 * HD])
             if not first:
                 r = r + jnp.concatenate([acc[0], acc[1, :, :2 * HD]], axis=1)
             if end:
@@ -598,15 +642,15 @@
                 acc[1, :, :2 * HD] = r[:, QW:]
 
         got(live, "p0")
-        qkv(me, True, False)
+        qkv([me], True, False)
+        got(live, "p1", "p2")
+        qkv([yn, xn], False, False)
         far(0, live[0])
-        got(live, "p2", "p3")
-        qkv(xn, False, False)
+        got(live, "p3", "p4")
+        qkv([xn, yn], False, False)
         far(1, live[1])
-        got(live, "p1", "p4")
-        qkv(yn, False, False)
         got(live, "p5", "p6")
-        qkv(dg, False, True)
+        qkv([dg], False, True)
         outs.append(pltpu.make_async_copy(qkv_v, qkv_hbm, isem.at[1]))
         outs[1].start()
         drain(live)

time: 150 us -> 147 us (0.980)
  Pallas kernels: 149 us -> 146 us
    pallas_call x2, Pallas kernels: 30.7 us -> 27.5 us  [attn_call(): pl.pallas_call(functools.partial(attn_kernel, layer, first), name=f'attn{...]
where the time goes in v6:
time: 147 us
  Pallas kernels  146 us (99%)
    pallas_call x2, Pallas kernels, mlp_call(): pl.pallas_call(functools.partial(mlp_kernel, layer, last), name=f'mlp{lay...  116 us
    pallas_call x2, Pallas kernels, attn_call(): pl.pallas_call(functools.partial(attn_kernel, layer, first), name=f'attn{...  27.5 us

profile of v6, /device:TPU:1, one launch (start us, length us, event | category | flops | bytes accessed | tf_op | source)
XLA Modules:
  0.0 146.6 jit_solution(17772282084076492679)
XLA Ops:
  0.6 15.3 %attn0.1 = (bf16[256,512]{1,0:T(8,128)(2,1)}, bf16[2,256,128,128]{3,2,1,0:T(8,128)(2,1)}, bf16[2,256,128,128]{3,2,1,0:T(8,128)(2,1)}) custom-call(s32[256]{0:T(256)} %pos_hbm.3, bf16[256,4096]{1,0:T(8,128)(2,1)} %x_hbm.3, bf16[2,4096]{1,0:T(2,128)(2,1)} %an_hbm.3, bf16[2,4096,512]{2,1,0:T(8,128)(2,1)} %wq_hbm.7, bf16[2,4096,128]{2,1,0:T(8,128)(2,1)} %wk_hbm.7, ...), custom_call_target="tpu_custom_call" | custom-call | tf_op jit(solution)/shard_map/attn0/pallas_call | solution.py:253
  15.9 60.1 %mlp0.1 = (bf16[2,256,256]{2,1,0:T(8,128)(2,1)}, bf16[256,768]{1,0:T(8,128)(2,1)}) custom-call(bf16[256,512]{1,0:T(8,128)(2,1)} %get-tuple-element.11.o_hbm, bf16[256,4096]{1,0:T(8,128)(2,1)} %x_hbm.3, bf16[2,4096]{1,0:T(2,128)(2,1)} %nw_hbm.7, bf16[2,4096]{1,0:T(2,128)(2,1)} %an_hbm.3, bf16[2,512,4096]{2,1,0:T(8,128)(2,1)} %wo_hbm.3, ...), custom_call_target="tpu_custom_call" | custom-call | tf_op jit(solution)/shard_map/mlp0/pallas_call | solution.py:670
  76.1 12.2 %attn1.1 = (bf16[256,512]{1,0:T(8,128)(2,1)}, bf16[2,256,128,128]{3,2,1,0:T(8,128)(2,1)}, bf16[2,256,128,128]{3,2,1,0:T(8,128)(2,1)}) custom-call(s32[256]{0:T(256)} %pos_hbm.3, bf16[256,768]{1,0:T(8,128)(2,1)} %get-tuple-element.12.x_hbm, bf16[2,4096]{1,0:T(2,128)(2,1)} %an_hbm.3, ...), custom_call_target="tpu_custom_call", output_to_operand_aliasing={{1}: (8, {}), {2}: (9, {})} | custom-call | tf_op jit(solution)/shard_map/attn1/pallas_call | solution.py:253
  88.3 55.7 %mlp1.1.x_hbm = bf16[256,4096]{1,0:T(8,128)(2,1)} custom-call(bf16[256,512]{1,0:T(8,128)(2,1)} %get-tuple-element.15.o_hbm, bf16[2,256,256]{2,1,0:T(8,128)(2,1)} %get-tuple-element.16.x_hbm, bf16[2,4096]{1,0:T(2,128)(2,1)} %nw_hbm.7, bf16[2,4096]{1,0:T(2,128)(2,1)} %an_hbm.3, bf16[2,512,4096]{2,1,0:T(8,128)(2,1)} %wo_hbm.3, bf16[2,4096,1792]{2,1,0:T(8,128)(2,1)} %wg_hbm.3, ...), custom_call_target="tpu_custom_call" | custom-call | tf_op jit(solution)/shard_map/mlp1/pallas_call | solution.py:670
  144.0 2.4 %emit.1 = bf16[256,4096]{1,0:T(8,128)(2,1)} custom-call(bf16[256,4096]{1,0:T(8,128)(2,1)} %mlp1.1.x_hbm), custom_call_target="tpu_custom_call" | custom-call | tf_op jit(solution)/shard_map/emit/pallas_call | solution.py:724

commit v7 on v6

--- a/solution.py
+++ b/solution.py
@@ -342,9 +342,11 @@
         wds.append(pltpu.make_async_copy(wd_hbm.at[layer, rs], wd_v.at[rs], wsem.at[2 * NG + i]))
     ocopy = pltpu.make_async_copy(o_hbm, o_ref, isem.at[0])
     ncopies = [pltpu.make_async_copy(nw_hbm, nw_ref, isem.at[1]), pltpu.make_async_copy(an_hbm, an_ref, isem.at[2])]
-    for t in [ocopy] + wos + ncopies + xcs:
+    for t in [ocopy] + wos[:2]:
         t.start()
     ocopy.wait()
+    for t in wos[2:] + ncopies + xcs:
+        t.start()
 
     def remote(src, dst, i, dev):
         return pltpu.make_async_remote_copy(src_ref=src, dst_ref=dst, send_sem=ssem.at[i], recv_sem=rsem.at[i],
@@ -366,9 +368,9 @@
             if t == 0:
                 c["a0"] = send(part.at[h, dg, top], r1.at[h, 0], NC * h + 4, xn)
                 c["b0"] = send(part.at[h, dg, bot], r1.at[h, 2], NC * h + 5, yn)
-            elif t == 1:
+            elif t == 1 and h == 0:
                 c["a1"] = send(part.at[h, xn, top], r1.at[h, 1], NC * h + 6, xn)
-            elif t == 2:
+            elif t == 2 and h == 0:
                 c["b1"] = send(part.at[h, yn, bot], r1.at[h, 3], NC * h + 7, yn)
 
         todo = []
@@ -391,6 +393,9 @@
             c["b0"].wait_recv()
             part[h, xn, bot] = (part[h, xn, bot].astype(F32) + r1[h, 2].astype(F32)).astype(BF16)
             c["b2"] = send(part.at[h, xn, bot], r2.at[h, 1], NC * h + 9, xn)
+            if h == 0:
+                live[1]["a1"] = send(part.at[1, xn, top], r1.at[1, 1], NC + 6, xn)
+                live[1]["b1"] = send(part.at[1, yn, bot], r1.at[1, 3], NC + 7, yn)
         return live
 
     def final(h, c):
@@ -583,7 +588,6 @@
         for h in range(2):
             final(h, live[h])
             gather_first(h, live[h])
-        for h in range(2):
             gather_second(h, live[h])
         for h in range(2):
             relay(h, live[h])

time: 147 us -> 148 us (level)
  no operation moved by 1% of the time
where the time goes in v7:
time: 148 us
  Pallas kernels  147 us (99%)
    pallas_call x2, Pallas kernels, mlp_call(): pl.pallas_call(functools.partial(mlp_kernel, layer, last), name=f'mlp{lay...  117 us
    pallas_call x2, Pallas kernels, attn_call(): pl.pallas_call(functools.partial(attn_kernel, layer, first), name=f'attn{...  27.5 us

profile of v7, /device:TPU:1, one launch (start us, length us, event | category | flops | bytes accessed | tf_op | source)
XLA Modules:
  0.0 147.6 jit_solution(4515114455299076458)
XLA Ops:
  0.6 15.3 %attn0.1 = (bf16[256,512]{1,0:T(8,128)(2,1)}, bf16[2,256,128,128]{3,2,1,0:T(8,128)(2,1)}, bf16[2,256,128,128]{3,2,1,0:T(8,128)(2,1)}) custom-call(s32[256]{0:T(256)} %pos_hbm.3, bf16[256,4096]{1,0:T(8,128)(2,1)} %x_hbm.3, bf16[2,4096]{1,0:T(2,128)(2,1)} %an_hbm.3, bf16[2,4096,512]{2,1,0:T(8,128)(2,1)} %wq_hbm.7, bf16[2,4096,128]{2,1,0:T(8,128)(2,1)} %wk_hbm.7, ...), custom_call_target="tpu_custom_call" | custom-call | tf_op jit(solution)/shard_map/attn0/pallas_call | solution.py:253
  15.9 61.3 %mlp0.1 = (bf16[2,256,256]{2,1,0:T(8,128)(2,1)}, bf16[256,768]{1,0:T(8,128)(2,1)}) custom-call(bf16[256,512]{1,0:T(8,128)(2,1)} %get-tuple-element.11.o_hbm, bf16[256,4096]{1,0:T(8,128)(2,1)} %x_hbm.3, bf16[2,4096]{1,0:T(2,128)(2,1)} %nw_hbm.7, bf16[2,4096]{1,0:T(2,128)(2,1)} %an_hbm.3, bf16[2,512,4096]{2,1,0:T(8,128)(2,1)} %wo_hbm.3, ...), custom_call_target="tpu_custom_call" | custom-call | tf_op jit(solution)/shard_map/mlp0/pallas_call | solution.py:674
  77.2 12.2 %attn1.1 = (bf16[256,512]{1,0:T(8,128)(2,1)}, bf16[2,256,128,128]{3,2,1,0:T(8,128)(2,1)}, bf16[2,256,128,128]{3,2,1,0:T(8,128)(2,1)}) custom-call(s32[256]{0:T(256)} %pos_hbm.3, bf16[256,768]{1,0:T(8,128)(2,1)} %get-tuple-element.12.x_hbm, bf16[2,4096]{1,0:T(2,128)(2,1)} %an_hbm.3, ...), custom_call_target="tpu_custom_call", output_to_operand_aliasing={{1}: (8, {}), {2}: (9, {})} | custom-call | tf_op jit(solution)/shard_map/attn1/pallas_call | solution.py:253
  89.4 55.6 %mlp1.1.x_hbm = bf16[256,4096]{1,0:T(8,128)(2,1)} custom-call(bf16[256,512]{1,0:T(8,128)(2,1)} %get-tuple-element.15.o_hbm, bf16[2,256,256]{2,1,0:T(8,128)(2,1)} %get-tuple-element.16.x_hbm, bf16[2,4096]{1,0:T(2,128)(2,1)} %nw_hbm.7, bf16[2,4096]{1,0:T(2,128)(2,1)} %an_hbm.3, bf16[2,512,4096]{2,1,0:T(8,128)(2,1)} %wo_hbm.3, bf16[2,4096,1792]{2,1,0:T(8,128)(2,1)} %wg_hbm.3, ...), custom_call_target="tpu_custom_call" | custom-call | tf_op jit(solution)/shard_map/mlp1/pallas_call | solution.py:674
  145.1 2.4 %emit.1 = bf16[256,4096]{1,0:T(8,128)(2,1)} custom-call(bf16[256,4096]{1,0:T(8,128)(2,1)} %mlp1.1.x_hbm), custom_call_target="tpu_custom_call" | custom-call | tf_op jit(solution)/shard_map/emit/pallas_call | solution.py:728

commit v8 on v6

--- a/solution.py
+++ b/solution.py
@@ -583,7 +583,6 @@
         for h in range(2):
             final(h, live[h])
             gather_first(h, live[h])
-        for h in range(2):
             gather_second(h, live[h])
         for h in range(2):
             relay(h, live[h])
@@ -615,18 +614,17 @@
     else:
         final(0, live[0])
         gather_first(0, live[0])
+        gather_second(0, live[0])
         final(1, live[1])
         sss = square_start()
         gather_first(1, live[1])
-        for h in range(2):
-            gather_second(h, live[h])
+        gather_second(1, live[1])
         outs = [pltpu.make_async_copy(xown, xo_hbm, isem.at[0])]
         outs[0].start()
         relay(0, live[0])
+        near(0, live[0])
         square_end(sss)
         relay(1, live[1])
-        for h in range(2):
-            near(h, live[h])
         for t in qs:
             t.wait()
 
@@ -643,6 +641,7 @@
 
         got(live, "p0")
         qkv([me], True, False)
+        near(1, live[1])
         got(live, "p1", "p2")
         qkv([yn, xn], False, False)
         far(0, live[0])

time: 147 us -> 146 us (level)
  no operation moved by 1% of the time
where the time goes in v8:
time: 146 us
  Pallas kernels  145 us (99%)
    pallas_call x2, Pallas kernels, mlp_call(): pl.pallas_call(functools.partial(mlp_kernel, layer, last), name=f'mlp{lay...  115 us
    pallas_call x2, Pallas kernels, attn_call(): pl.pallas_call(functools.partial(attn_kernel, layer, first), name=f'attn{...  27.5 us

profile of v8, /device:TPU:1, one launch (start us, length us, event | category | flops | bytes accessed | tf_op | source)
XLA Modules:
  0.0 145.5 jit_solution(1968739388895938996)
XLA Ops:
  0.6 15.3 %attn0.1 = (bf16[256,512]{1,0:T(8,128)(2,1)}, bf16[2,256,128,128]{3,2,1,0:T(8,128)(2,1)}, bf16[2,256,128,128]{3,2,1,0:T(8,128)(2,1)}) custom-call(s32[256]{0:T(256)} %pos_hbm.3, bf16[256,4096]{1,0:T(8,128)(2,1)} %x_hbm.3, bf16[2,4096]{1,0:T(2,128)(2,1)} %an_hbm.3, bf16[2,4096,512]{2,1,0:T(8,128)(2,1)} %wq_hbm.7, bf16[2,4096,128]{2,1,0:T(8,128)(2,1)} %wk_hbm.7, ...), custom_call_target="tpu_custom_call" | custom-call | tf_op jit(solution)/shard_map/attn0/pallas_call | solution.py:253
  15.9 59.6 %mlp0.1 = (bf16[2,256,256]{2,1,0:T(8,128)(2,1)}, bf16[256,768]{1,0:T(8,128)(2,1)}) custom-call(bf16[256,512]{1,0:T(8,128)(2,1)} %get-tuple-element.11.o_hbm, bf16[256,4096]{1,0:T(8,128)(2,1)} %x_hbm.3, bf16[2,4096]{1,0:T(2,128)(2,1)} %nw_hbm.7, bf16[2,4096]{1,0:T(2,128)(2,1)} %an_hbm.3, bf16[2,512,4096]{2,1,0:T(8,128)(2,1)} %wo_hbm.3, ...), custom_call_target="tpu_custom_call" | custom-call | tf_op jit(solution)/shard_map/mlp0/pallas_call | solution.py:669
  75.5 12.2 %attn1.1 = (bf16[256,512]{1,0:T(8,128)(2,1)}, bf16[2,256,128,128]{3,2,1,0:T(8,128)(2,1)}, bf16[2,256,128,128]{3,2,1,0:T(8,128)(2,1)}) custom-call(s32[256]{0:T(256)} %pos_hbm.3, bf16[256,768]{1,0:T(8,128)(2,1)} %get-tuple-element.12.x_hbm, bf16[2,4096]{1,0:T(2,128)(2,1)} %an_hbm.3, ...), custom_call_target="tpu_custom_call", output_to_operand_aliasing={{1}: (8, {}), {2}: (9, {})} | custom-call | tf_op jit(solution)/shard_map/attn1/pallas_call | solution.py:253
  87.7 55.2 %mlp1.1.x_hbm = bf16[256,4096]{1,0:T(8,128)(2,1)} custom-call(bf16[256,512]{1,0:T(8,128)(2,1)} %get-tuple-element.15.o_hbm, bf16[2,256,256]{2,1,0:T(8,128)(2,1)} %get-tuple-element.16.x_hbm, bf16[2,4096]{1,0:T(2,128)(2,1)} %nw_hbm.7, bf16[2,4096]{1,0:T(2,128)(2,1)} %an_hbm.3, bf16[2,512,4096]{2,1,0:T(8,128)(2,1)} %wo_hbm.3, bf16[2,4096,1792]{2,1,0:T(8,128)(2,1)} %wg_hbm.3, ...), custom_call_target="tpu_custom_call" | custom-call | tf_op jit(solution)/shard_map/mlp1/pallas_call | solution.py:669
  142.9 2.4 %emit.1 = bf16[256,4096]{1,0:T(8,128)(2,1)} custom-call(bf16[256,4096]{1,0:T(8,128)(2,1)} %mlp1.1.x_hbm), custom_call_target="tpu_custom_call" | custom-call | tf_op jit(solution)/shard_map/emit/pallas_call | solution.py:723

commit v9 on v8

--- a/solution.py
+++ b/solution.py
@@ -503,11 +503,11 @@
         t.wait()
     final(0, live[0])
     gather_first(0, live[0])
+    gather_second(0, live[0])
     final(1, live[1])
     sss = square_start()
     gather_first(1, live[1])
-    for h in range(2):
-        gather_second(h, live[h])
+    gather_second(1, live[1])
     relay(0, live[0])
     square_end(sss)
     relay(1, live[1])

time: 146 us -> 149 us (1.021)
  Pallas kernels: 145 us -> 148 us
    pallas_call x2, Pallas kernels: 115 us -> 118 us  [mlp_call(): pl.pallas_call(functools.partial(mlp_kernel, layer, last), name=f'mlp{lay...]
where the time goes in v9:
time: 149 us
  Pallas kernels  148 us (99%)
    pallas_call x2, Pallas kernels, mlp_call(): pl.pallas_call(functools.partial(mlp_kernel, layer, last), name=f'mlp{lay...  118 us
    pallas_call x2, Pallas kernels, attn_call(): pl.pallas_call(functools.partial(attn_kernel, layer, first), name=f'attn{...  27.5 us

profile of v9, /device:TPU:1, one launch (start us, length us, event | category | flops | bytes accessed | tf_op | source)
XLA Modules:
  0.0 148.5 jit_solution(3602733155260463904)
XLA Ops:
  0.6 15.3 %attn0.1 = (bf16[256,512]{1,0:T(8,128)(2,1)}, bf16[2,256,128,128]{3,2,1,0:T(8,128)(2,1)}, bf16[2,256,128,128]{3,2,1,0:T(8,128)(2,1)}) custom-call(s32[256]{0:T(256)} %pos_hbm.3, bf16[256,4096]{1,0:T(8,128)(2,1)} %x_hbm.3, bf16[2,4096]{1,0:T(2,128)(2,1)} %an_hbm.3, bf16[2,4096,512]{2,1,0:T(8,128)(2,1)} %wq_hbm.7, bf16[2,4096,128]{2,1,0:T(8,128)(2,1)} %wk_hbm.7, ...), custom_call_target="tpu_custom_call" | custom-call | tf_op jit(solution)/shard_map/attn0/pallas_call | solution.py:253
  15.9 61.0 %mlp0.1 = (bf16[2,256,256]{2,1,0:T(8,128)(2,1)}, bf16[256,768]{1,0:T(8,128)(2,1)}) custom-call(bf16[256,512]{1,0:T(8,128)(2,1)} %get-tuple-element.11.o_hbm, bf16[256,4096]{1,0:T(8,128)(2,1)} %x_hbm.3, bf16[2,4096]{1,0:T(2,128)(2,1)} %nw_hbm.7, bf16[2,4096]{1,0:T(2,128)(2,1)} %an_hbm.3, bf16[2,512,4096]{2,1,0:T(8,128)(2,1)} %wo_hbm.3, ...), custom_call_target="tpu_custom_call" | custom-call | tf_op jit(solution)/shard_map/mlp0/pallas_call | solution.py:669
  76.9 12.2 %attn1.1 = (bf16[256,512]{1,0:T(8,128)(2,1)}, bf16[2,256,128,128]{3,2,1,0:T(8,128)(2,1)}, bf16[2,256,128,128]{3,2,1,0:T(8,128)(2,1)}) custom-call(s32[256]{0:T(256)} %pos_hbm.3, bf16[256,768]{1,0:T(8,128)(2,1)} %get-tuple-element.12.x_hbm, bf16[2,4096]{1,0:T(2,128)(2,1)} %an_hbm.3, ...), custom_call_target="tpu_custom_call", output_to_operand_aliasing={{1}: (8, {}), {2}: (9, {})} | custom-call | tf_op jit(solution)/shard_map/attn1/pallas_call | solution.py:253
  89.1 56.8 %mlp1.1.x_hbm = bf16[256,4096]{1,0:T(8,128)(2,1)} custom-call(bf16[256,512]{1,0:T(8,128)(2,1)} %get-tuple-element.15.o_hbm, bf16[2,256,256]{2,1,0:T(8,128)(2,1)} %get-tuple-element.16.x_hbm, bf16[2,4096]{1,0:T(2,128)(2,1)} %nw_hbm.7, bf16[2,4096]{1,0:T(2,128)(2,1)} %an_hbm.3, bf16[2,512,4096]{2,1,0:T(8,128)(2,1)} %wo_hbm.3, bf16[2,4096,1792]{2,1,0:T(8,128)(2,1)} %wg_hbm.3, ...), custom_call_target="tpu_custom_call" | custom-call | tf_op jit(solution)/shard_map/mlp1/pallas_call | solution.py:669
  145.9 2.4 %emit.1 = bf16[256,4096]{1,0:T(8,128)(2,1)} custom-call(bf16[256,4096]{1,0:T(8,128)(2,1)} %mlp1.1.x_hbm), custom_call_target="tpu_custom_call" | custom-call | tf_op jit(solution)/shard_map/emit/pallas_call | solution.py:723
